TPU v7x, 32 devices: a whole 2x2x4 slice. The times are simulated.
32 devices in a mesh: groups: 2 (over y), az: 4 (over z), rg: 2 (over x), acq: 2 (over core).
Axes of the slice: x: 2, y: 2, z: 4, core: 2. Of those that a mesh axis runs over, the one named last changes fastest.
Arguments:
- image_stack: bfloat16 [2, 64, 32, 4, 256], P(None, ('az', 'acq'), 'groups', 'rg'), parts along dimension 2, may hold values from -12 to 12
- steering: bfloat16 [4, 2, 64, 512], P('rg'), as said below
- wiener_filter: bfloat16 [4, 2, 64, 64], P('rg'), may hold values from -0.5 to 0.5
- range_group: int32 [4], P('rg'), may hold values from 0 to 3, as said below
- lay_list: int32 [32, 4, 32], P(('groups', 'az', 'acq'), 'rg'), parts along dimension 0, may hold values from 0 to 255, as said below
- lay_count: int32 [32, 4], P(('groups', 'az', 'acq'), 'rg'), parts along dimension 0, may hold values from 0 to 32, as said below
Outputs:
- power: bfloat16 [32, 4, 512, 256], P(('groups', 'az', 'acq'), 'rg'), parts along dimension 0
There are 2 independent parts, one for each index of `groups`. A program takes and returns all parts, laid end to end along the dimension named above; an argument that names none is the same for every part. Nothing has to cross between parts.
Inputs may be any that keep to these rules, and one draw needn't show every extreme that they name: `lay_list`: within one block the 32 entries are distinct pixels. The first lay_count entries of a block's list are its layover pixels; some block has 32. `range_group`: range block r belongs to a group from (r // 2) * 2 to (r // 2) * 2 + 1. `steering`: every complex entry has modulus 1 / sqrt(512) up to rounding.
All inputs are finite; a program needn't handle non-finite values.
Results may differ from a plain program's by a relative error of at most 0.0075.
Values may be sent and summed in bfloat16 or wider, within the bound.
No kernel may reach another device: no remote copies, remote signals or barrier semaphores. Data moves between devices by JAX's collectives and lax.ppermute only.
A program may use at most 64 MiB of HBM per device.

v0:
```python
import jax
import jax.numpy as jnp
from jax import lax
from jax.experimental import pallas as pl
from jax.experimental.pallas import tpu as pltpu
from jax.sharding import PartitionSpec as P

ITERS = 8
STEP_SIZE = 0.5
SHRINK = 0.25
LANES = 128
WIENER_ROWS = 128
F32 = jnp.float32
BF16 = jnp.bfloat16

VMEM = pl.BlockSpec(memory_space=pltpu.VMEM)
SMEM = pl.BlockSpec(memory_space=pltpu.SMEM)
ANY = pl.BlockSpec(memory_space=pl.ANY)


def dot(a, b, contract=(1, 0)):
    return lax.dot_general(
        a, b, (((contract[0],), (contract[1],)), ((), ())), preferred_element_type=F32
    )


def relay_kernel(places, x_ref, *refs):
    chunks, sem = refs[:-1], refs[-1]
    halves, acq_share = x_ref.shape[:2]
    chip, core = lax.axis_index("az"), lax.axis_index("acq")
    cores = lax.axis_size("acq")
    copies = []
    for owners, chunk in zip(places, chunks):
        blocks = chunk.shape[0] // len(owners)
        for at, (d, j) in enumerate(owners):
            first = ((chip ^ d) * cores + (core ^ j)) * blocks
            for half in range(halves):
                for acq in range(acq_share):
                    copies.append(
                        pltpu.make_async_copy(
                            x_ref.at[half, acq, pl.ds(first, blocks)],
                            chunk.at[pl.ds(at * blocks, blocks), half, :, acq],
                            sem,
                        )
                    )
    for copy in copies:
        copy.start()
    for copy in copies:
        copy.wait()


def prepare_kernel(
    acq_share, relative, groups, counts, list_ref, steer_ref, filter_ref,
    first_ref, half_op_ref, op_t_ref, wiener_ref, select_ref, chosen_ref, clear_ref, fmat_ref,
):
    acquisitions, _ = steer_ref.shape[2:]
    blocks, columns = counts.shape
    depth = 2 * acquisitions
    pixels = chosen_ref.shape[1]
    entries = list_ref.shape[1]
    per_block = entries // (blocks * columns)
    lane = lax.broadcasted_iota(jnp.int32, (1, entries), 1)
    limit = jnp.zeros((1, entries), jnp.int32)
    for a in range(blocks):
        for r in range(columns):
            start = (a * columns + r) * per_block
            inside = (lane >= start) & (lane < start + per_block)
            limit = jnp.where(inside, counts[a, r] + start, limit)
    listed = jnp.where(lane < limit, list_ref[...], -1)
    hits = lax.broadcasted_iota(jnp.int32, (pixels, entries), 0) == listed
    chosen = jnp.transpose(jnp.where(hits, 1.0, 0.0).astype(F32))
    chosen_ref[...] = chosen.astype(BF16)
    for a in range(blocks):
        for r in range(columns):
            start = (a * columns + r) * per_block
            covered = jnp.sum(chosen[start : start + per_block], axis=0, keepdims=True)
            clear_ref[a * columns + r] = jnp.broadcast_to(1.0 - covered, clear_ref.shape[1:])
    row = lax.broadcasted_iota(jnp.int32, (columns * depth, depth), 0)
    column_at = lax.broadcasted_iota(jnp.int32, (columns * depth, depth), 1)
    for r in range(columns):
        g = groups[r] - lax.axis_index("rg") * steer_ref.shape[0]
        pair = row // columns
        acq = pair % acq_share
        half = (pair // acq_share) % 2
        source = pair // (2 * acq_share)
        if relative:
            cores = lax.axis_size("acq")
            chip, core = lax.axis_index("az"), lax.axis_index("acq")
            source = ((source // cores) ^ chip) * cores + ((source % cores) ^ core)
        target = half * acquisitions + source * acq_share + acq
        hit = (column_at == target) & (row % columns == r)
        select = jnp.where(hit, 1.0, 0.0).astype(BF16)
        select_ref[r] = select
        real = steer_ref[g, 0]
        imag = steer_ref[g, 1]
        operator = jnp.concatenate(
            [
                jnp.concatenate([real, -imag], axis=1),
                jnp.concatenate([imag, real], axis=1),
            ],
            axis=0,
        )
        half_op = operator * jnp.asarray(STEP_SIZE, BF16)
        half_op_ref[r] = half_op
        first_ref[r] = dot(select, half_op).astype(BF16)
        op_t = jnp.transpose(operator.astype(F32)).astype(BF16)
        op_t_ref[r] = op_t
        fmat_ref[:acquisitions, :acquisitions] = filter_ref[g, 0].astype(F32)
        fmat_ref[:acquisitions, acquisitions:] = -filter_ref[g, 1].astype(F32)
        fmat_ref[acquisitions:, :acquisitions] = filter_ref[g, 1].astype(F32)
        fmat_ref[acquisitions:, acquisitions:] = filter_ref[g, 0].astype(F32)
        beam = dot(op_t, fmat_ref[...].astype(BF16)).astype(BF16)
        wiener_ref[r] = dot(beam, select, (1, 1)).astype(BF16)


def profile_body(
    grid, first_ref, half_op_ref, op_t_ref, wiener_ref, select_ref, chosen_ref, clear_ref,
    out_ref, real_ref, imag_ref, rounded_ref, target_ref, image_ref, sem,
):
    blocks, columns, elevation, _ = out_ref.shape
    per_block = chosen_ref.shape[0] // (blocks * columns)
    picked = [
        dot(
            chosen_ref[a * columns * per_block : (a + 1) * columns * per_block],
            grid(a),
            (1, 1),
        ).astype(BF16)
        for a in range(blocks)
    ]
    picked = [
        jnp.concatenate([p[r * per_block : (r + 1) * per_block] for p in picked], axis=0)
        for r in range(columns)
    ]
    for r in range(columns):
        target_ref[r] = dot(picked[r], select_ref[r])

    tile = 256

    def update(r, misfit, op_ref, first):
        for at in range(0, elevation, tile):
            zr = dot(misfit, op_ref[r, :, at : at + tile])
            zi = dot(misfit, op_ref[r, :, elevation + at : elevation + at + tile])
            if not first:
                zr = zr + real_ref[r, :, at : at + tile]
                zi = zi + imag_ref[r, :, at : at + tile]
            magnitude = zr * zr + zi * zi
            factor = jnp.maximum(
                1.0 - SHRINK * lax.rsqrt(jnp.maximum(magnitude, SHRINK * SHRINK)), 0.0
            )
            xr = zr * factor
            xi = zi * factor
            real_ref[r, :, at : at + tile] = xr
            imag_ref[r, :, at : at + tile] = xi
            rounded_ref[r, :, at : at + tile] = xr.astype(BF16)
            rounded_ref[r, :, elevation + at : elevation + at + tile] = xi.astype(BF16)

    shares = [(a, r, at) for a in range(blocks) for at in range(0, elevation, WIENER_ROWS)
              for r in range(columns)]

    def wiener(a, r, at):
        br = dot(wiener_ref[r, at : at + WIENER_ROWS], grid(a))
        bi = dot(wiener_ref[r, elevation + at : elevation + at + WIENER_ROWS], grid(a))
        power = (br * br + bi * bi) * clear_ref[a * columns + r, :1]
        image_ref[a, r, at : at + WIENER_ROWS] = power.astype(BF16)

    done = 0
    for t in range(ITERS):
        for r in range(columns):
            if t == 0:
                update(r, picked[r], first_ref, True)
            else:
                misfit = (target_ref[r] - dot(rounded_ref[r], op_t_ref[r])).astype(BF16)
                update(r, misfit, half_op_ref, False)
        until = len(shares) * (t + 1) // ITERS
        for share in shares[done:until]:
            wiener(*share)
        done = until

    for r in range(columns):
        for a in range(blocks):
            start = (a * columns + r) * per_block
            chosen = chosen_ref[start : start + per_block]
            xr = real_ref[r, a * per_block : (a + 1) * per_block]
            xi = imag_ref[r, a * per_block : (a + 1) * per_block]
            strength = (xr * xr + xi * xi).astype(BF16)
            placed = dot(strength, chosen, (0, 0)).astype(BF16)
            image_ref[a, r] = image_ref[a, r] + placed
            pltpu.make_async_copy(image_ref.at[a, r], out_ref.at[a, r], sem).start()
    for a in range(blocks):
        for r in range(columns):
            pltpu.make_async_copy(image_ref.at[a, r], out_ref.at[a, r], sem).wait()


def join_kernel(skips, *refs):
    out_ref = refs[-1]
    at = 0
    for skip, ref in zip(skips, refs[:-1]):
        size = ref.shape[0] - skip
        out_ref[at : at + size] = ref[skip:]
        at += size


def pieces_kernel(count, order, *refs):
    pieces, rest = refs[:count], refs[count:]

    def grid(a):
        rows = []
        for at, lead in order:
            ref = pieces[at]
            where = lead + (a,) if len(ref.shape) == 6 else (a,)
            halves, tiles = ref.shape[-4:-2]
            for half in range(halves):
                rows.append(
                    jnp.concatenate(
                        [ref[where + (half, t)] for t in range(tiles)], axis=1
                    )
                )
        return jnp.concatenate(rows, axis=0)

    profile_body(grid, *rest)


def plain_kernel(pieces, *rest):
    profile_body(lambda a: pieces[a], *rest)


def shards(image_stack, steering, wiener_filter, range_group, lay_list, lay_count):
    halves, acq_share, azb_all, columns, pixels = image_stack.shape
    blocks = lay_list.shape[0]
    _, _, acquisitions, elevation = steering.shape
    depth = 2 * acquisitions
    chips = lax.axis_size("az")
    cores = lax.axis_size("acq")
    per_block = lay_list.shape[2]
    rows = blocks * per_block
    tiles = pixels // LANES
    pairwise = acq_share * columns == 16 and cores == 2 and chips & (chips - 1) == 0
    prepared = pl.pallas_call(
        lambda *refs: prepare_kernel(acq_share, pairwise, *refs),
        out_shape=[
            jax.ShapeDtypeStruct((columns, columns * depth, 2 * elevation), BF16),
            jax.ShapeDtypeStruct((columns, depth, 2 * elevation), BF16),
            jax.ShapeDtypeStruct((columns, 2 * elevation, depth), BF16),
            jax.ShapeDtypeStruct((columns, 2 * elevation, columns * depth), BF16),
            jax.ShapeDtypeStruct((columns, columns * depth, depth), BF16),
            jax.ShapeDtypeStruct((blocks * columns * per_block, pixels), BF16),
            jax.ShapeDtypeStruct((blocks * columns, 8, pixels), F32),
        ],
        in_specs=[SMEM, SMEM, VMEM, VMEM, VMEM],
        out_specs=[VMEM] * 7,
        scratch_shapes=[pltpu.VMEM((depth, depth), F32)],
        cost_estimate=pl.CostEstimate(
            flops=1_000_000_000, bytes_accessed=4_000_000, transcendentals=0
        ),
        compiler_params=pltpu.CompilerParams(vmem_limit_bytes=16 << 20),
        name="prepare",
    )(range_group, lay_count, lay_list.reshape(1, -1), steering, wiener_filter)

    if pairwise:
        view = image_stack.reshape(halves, acq_share, azb_all, columns, tiles, LANES)
        view = view.transpose(0, 1, 2, 4, 3, 5)
        far = chips - 1
        turns = sorted(range(1, chips), key=lambda d: (d < chips // 2, d))
        places = [[(0, 0)], [(0, 1)]]
        for d in turns:
            places += [[(d, 0)], [(d, 1)]] if d == far else [[(d, 0), (d, 1)]]
        unit = (halves, tiles, acq_share, columns, LANES)
        chunks = pl.pallas_call(
            lambda *refs: relay_kernel(places, *refs),
            out_shape=[
                jax.ShapeDtypeStruct((len(owners) * blocks,) + unit, BF16)
                for owners in places
            ],
            in_specs=[ANY],
            out_specs=[VMEM] * len(places),
            scratch_shapes=[pltpu.SemaphoreType.DMA],
            compiler_params=pltpu.CompilerParams(vmem_limit_bytes=2 << 20),
            name="relay",
        )(view)
        flat = (halves, tiles, acq_share * columns, LANES)
        chunks = [chunk.reshape((-1,) + flat) for chunk in chunks]
        got, waiting = {(0, 0): chunks[0]}, [((0, 1), chunks[1])]
        for owners, chunk in zip(places[2:], chunks[2:]):
            d, j = owners[0]
            straight = [
                (c * cores + q, (c ^ d) * cores + (q ^ j))
                for c in range(chips)
                for q in range(cores)
            ]
            arrived = lax.ppermute(chunk, ("az", "acq"), straight)
            got[d, j] = arrived
            if len(owners) == 2:
                waiting.append(((d, 1), arrived))
        skips = [w.shape[0] - blocks for _, w in waiting]
        passing = pl.pallas_call(
            lambda *refs: join_kernel(skips, *refs),
            out_shape=jax.ShapeDtypeStruct((len(waiting) * blocks,) + flat, BF16),
            in_specs=[VMEM] * len(waiting),
            out_specs=VMEM,
            compiler_params=pltpu.CompilerParams(vmem_limit_bytes=2 << 20),
            name="join",
        )(*[w for _, w in waiting])
        passing, prepared = lax.optimization_barrier((passing, prepared))
        passed = lax.ppermute(passing, "acq", [(0, 1), (1, 0)])
        arrays, order = [], {}
        for place, array in got.items():
            order[place] = (len(arrays), ())
            arrays.append(array)
        for at, (place, _) in enumerate(waiting):
            order[place] = (len(arrays), (at,))
        arrays.append(passed.reshape((len(waiting), blocks) + flat))
        order = [order[d, j] for d in range(chips) for j in range(cores)]
        lead = arrays
        body = lambda *refs: pieces_kernel(len(arrays), order, *refs)
    else:
        moved = lax.all_to_all(
            image_stack, ("az", "acq"), split_axis=2, concat_axis=0, tiled=True
        )
        moved = moved.reshape(-1, acq_share, blocks, columns, pixels)
        lead = [moved.transpose(2, 0, 1, 3, 4).reshape(blocks, columns * depth, pixels)]
        body = plain_kernel

    return pl.pallas_call(
        body,
        out_shape=jax.ShapeDtypeStruct((blocks, columns, elevation, pixels), BF16),
        in_specs=[VMEM] * (len(lead) + len(prepared)),
        out_specs=ANY,
        scratch_shapes=[
            pltpu.VMEM((columns, rows, elevation), F32),
            pltpu.VMEM((columns, rows, elevation), F32),
            pltpu.VMEM((columns, rows, 2 * elevation), BF16),
            pltpu.VMEM((columns, rows, depth), F32),
            pltpu.VMEM((blocks, columns, elevation, pixels), BF16),
            pltpu.SemaphoreType.DMA,
        ],
        compiler_params=pltpu.CompilerParams(vmem_limit_bytes=24 << 20),
        cost_estimate=pl.CostEstimate(
            flops=2_000_000_000, bytes_accessed=4_000_000, transcendentals=0
        ),
        name="profiles",
    )(*lead, *prepared)


def solution(mesh):
    return jax.shard_map(
        shards,
        mesh=mesh,
        in_specs=(
            P(None, ("az", "acq"), "groups", "rg", None),
            P("rg", None, None, None),
            P("rg", None, None, None),
            P("rg"),
            P(("groups", "az", "acq"), "rg", None),
            P(("groups", "az", "acq"), "rg"),
        ),
        out_specs=P(("groups", "az", "acq"), "rg", None, None),
        check_vma=False,
    )
```

profile of v0, /device:TPU:0, one launch (start us, length us, event | category | flops | bytes accessed | tf_op | source)
XLA Modules:
  0.0 23.0 jit_solution(13909392519427332887)
XLA Ops:
  0.0 0.0 copy-start
  0.0 0.9 %copy-done = bf16[2,8,16,2,256]{4,3,2,1,0:T(2,128)(2,1)S(1)} copy-done((bf16[2,8,16,2,256]{4,3,2,1,0:T(2,128)(2,1)S(1)}, bf16[2,8,16,2,256]{4,3,2,1,0:T(2,128)(2,1)}, u32[]{:S(2)}) %copy-start) | copy-done | bytes 262168
  1.0 0.0 copy-start.1
  1.0 0.3 %relay.1 = (bf16[2,2,2,8,2,128]{5,4,3,2,1,0:T(2,128)(2,1)S(1)}, bf16[2,2,2,8,2,128]{5,4,3,2,1,0:T(2,128)(2,1)S(1)}, bf16[4,2,2,8,2,128]{5,4,3,2,1,0:T(2,128)(2,1...) custom-call(bf16[2,8,16,2,2,128]{5,4,3,2,1,0:T(2,128)(2,1)S(1)} %bit, ...), custom_call_target="tpu_custom_call" | custom-call | tf_op jit(solution)/shard_map/relay/pallas_call | solution.py:268
  1.2 0.0 copy-start.5
  1.3 4.1 %collective-permute-start = (bf16[4,2,2,16,128]{4,3,2,1,0:T(8,128)(2,1)S(1)}, bf16[4,2,2,16,128]{4,3,2,1,0:T(8,128)(2,1)S(1)}, u32[]{:S(2)}, u32[]{:S(2)}) collective-permute-start(bf16[4,2,2,16,128]{4,3,2,1,0:T(8,128)(2,1)S(1)} %bitcast.14), channel_id=1, source_target_pairs={{0,8},{1,9},{4,12},{5,13},{8,0},{9,1},{12,4},{13,5},{2,10},{3,11},... | collective-permute-start | bytes 196616 | tf_op jit(solution)/shard_map/ppermute | solution.py:290
  5.4 0.0 copy-start.3
  5.4 0.0 copy-start.4
  5.4 1.6 %collective-permute-start.3 = (bf16[4,2,2,16,128]{4,3,2,1,0:T(8,128)(2,1)S(1)}, bf16[4,2,2,16,128]{4,3,2,1,0:T(8,128)(2,1)S(1)}, u32[]{:S(2)}, u32[]{:S(2)}) collective-permute-start(bf16[4,2,2,16,128]{4,3,2,1,0:T(8,128)(2,1)S(1)} %bitcast.13), channel_id=1, source_target_pairs={{0,4},{1,5},{4,0},{5,1},{8,12},{9,13},{12,8},{13,9},{2,6},{3,7},{6... | collective-permute-start | bytes 196616 | tf_op jit(solution)/shard_map/ppermute | solution.py:290
  7.0 0.0 copy-done.5
  7.0 0.1 reshape.34.refs_2_
  7.0 0.0 copy-done.1
  7.1 0.0 copy-done.3
  7.1 0.0 copy-done.4
  7.1 0.0 copy-start.2
  7.1 0.8 %copy-done.2 = bf16[2,2,64,64]{3,2,1,0:T(8,128)(2,1)S(1)} copy-done((bf16[2,2,64,64]{3,2,1,0:T(8,128)(2,1)S(1)}, bf16[2,2,64,64]{3,2,1,0:T(8,128)(2,1)}, u32[]{:S(2)}) %copy-start.2) | copy-done | bytes 32792
  7.9 1.7 %prepare.1 = (bf16[2,256,1024]{2,1,0:T(8,128)(2,1)S(1)}, bf16[2,128,1024]{2,1,0:T(8,128)(2,1)S(1)}, bf16[2,1024,128]{2,1,0:T(8,128)(2,1)S(1)}, bf16[2,1024,256]{...) custom-call(s32[2]{0:T(128)S(1)} %copy-done.4, ...), custom_call_target="tpu_custom_call" | custom-call | flops 1000000000 | bytes 4000000 | tf_op jit(solution)/shard_map/prepare/pallas_call | solution.py:238
  9.6 0.0 collective-permute-done.refs_1_
  9.7 0.0 collective-permute-done.3.refs_2_.refs_4_
  9.7 0.1 collective-permute-start.4
  9.8 2.8 %collective-permute-start.1 = (bf16[2,2,2,16,128]{4,3,2,1,0:T(8,128)(2,1)S(1)}, bf16[2,2,2,16,128]{4,3,2,1,0:T(8,128)(2,1)S(1)}, u32[]{:S(2)}, u32[]{:S(2)}) collective-permute-start(bf16[2,2,2,16,128]{4,3,2,1,0:T(8,128)(2,1)S(1)} %bitcast.17), channel_id=1, source_target_pairs={{0,12},{1,13},{4,8},{5,9},{8,4},{9,5},{12,0},{13,1},{2,14},{3,15},... | collective-permute-start | bytes 98312 | tf_op jit(solution)/shard_map/ppermute | solution.py:290
  12.6 0.8 %collective-permute-start.2 = (bf16[2,2,2,16,128]{4,3,2,1,0:T(8,128)(2,1)S(1)}, bf16[2,2,2,16,128]{4,3,2,1,0:T(8,128)(2,1)S(1)}, u32[]{:S(2)}, u32[]{:S(2)}) collective-permute-start(bf16[2,2,2,16,128]{4,3,2,1,0:T(8,128)(2,1)S(1)} %bitcast.16), channel_id=1, source_target_pairs={{0,13},{1,12},{4,9},{5,8},{8,5},{9,4},{12,1},{13,0},{2,15},{3,14},... | collective-permute-start | bytes 98312 | tf_op jit(solution)/shard_map/ppermute | solution.py:290
  13.4 2.1 %collective-permute-done.1.refs_2_ = bf16[2,2,2,16,128]{4,3,2,1,0:T(8,128)(2,1)S(1)} collective-permute-done((bf16[2,2,2,16,128]{4,3,2,1,0:T(8,128)(2,1)S(1)}, bf16[2,2,2,16,128]{4,3,2,1,0:T(8,128)(2,1)S(1)}, u32[]{:S(2)}, u32[]{:S(2)}) %collective-permute-start.1) | collective-permute-done | bytes 32800 | tf_op jit(solution)/shard_map/ppermute | solution.py:290
  15.5 2.2 %collective-permute-done.2.refs_3_ = bf16[2,2,2,16,128]{4,3,2,1,0:T(8,128)(2,1)S(1)} collective-permute-done((bf16[2,2,2,16,128]{4,3,2,1,0:T(8,128)(2,1)S(1)}, bf16[2,2,2,16,128]{4,3,2,1,0:T(8,128)(2,1)S(1)}, u32[]{:S(2)}, u32[]{:S(2)}) %collective-permute-start.2) | collective-permute-done | bytes 32800 | tf_op jit(solution)/shard_map/ppermute | solution.py:290
  17.7 0.0 collective-permute-done.4
  17.7 5.3 %profiles.1 = bf16[2,2,512,256]{3,2,1,0:T(8,128)(2,1)} custom-call(bf16[2,2,2,16,128]{4,3,2,1,0:T(8,128)(2,1)S(1)} %bitcast.15, bf16[4,2,2,16,128]{4,3,2,1,0:T(8,128)(2,1)S(1)} %collective-permute-done.refs_1_, bf16[2,2,2,16,128]{4,3,2,1,0:T(8,128)(2,1)S(1)} %collective-permute-done.1.refs_2_, ...), custom_call_target="tpu_custom_call" | custom-call | flops 2000000000 | bytes 4000000 | tf_op jit(solution)/shard_map/profiles/pallas_call | solution.py:323
  (1 shorter events, 0.0 us)
Async XLA Ops:
  0.0 0.9 %copy-start = (bf16[2,8,16,2,256]{4,3,2,1,0:T(2,128)(2,1)S(1)}, bf16[2,8,16,2,256]{4,3,2,1,0:T(2,128)(2,1)}, u32[]{:S(2)}) copy-start(bf16[2,8,16,2,256]{4,3,2,1,0:T(2,128)(2,1)} %param.6) | copy-start | bytes 786436
  1.0 6.1 %copy-start.1 = (bf16[2,2,64,512]{3,2,1,0:T(8,128)(2,1)S(1)}, bf16[2,2,64,512]{3,2,1,0:T(8,128)(2,1)}, u32[]{:S(2)}) copy-start(bf16[2,2,64,512]{3,2,1,0:T(8,128)(2,1)} %refs_3_.1) | copy-start | bytes 786436
  1.2 5.7 %copy-start.5 = (s32[2,2,32]{2,1,0:T(2,128)S(1)}, s32[2,2,32]{2,1,0:T(2,128)}, u32[]{:S(2)}) copy-start(s32[2,2,32]{2,1,0:T(2,128)} %param.10) | copy-start | bytes 1540
  1.3 8.4 %collective-permute-start = (bf16[4,2,2,16,128]{4,3,2,1,0:T(8,128)(2,1)S(1)}, bf16[4,2,2,16,128]{4,3,2,1,0:T(8,128)(2,1)S(1)}, u32[]{:S(2)}, u32[]{:S(2)}) collective-permute-start(bf16[4,2,2,16,128]{4,3,2,1,0:T(8,128)(2,1)S(1)} %bitcast.14), channel_id=1, source_target_pairs={{0,8},{1,9},{4,12},{5,13},{8,0},{9,1},{12,4},{13,5},{2,10},{3,11},... | collective-permute-start | bytes 196616 | tf_op jit(solution)/shard_map/ppermute | solution.py:290
  5.4 1.7 %copy-start.3 = (s32[2,2]{1,0:T(2,128)S(1)}, s32[2,2]{1,0:T(2,128)}, u32[]{:S(2)}) copy-start(s32[2,2]{1,0:T(2,128)} %refs_1_.1) | copy-start | bytes 52
  5.4 1.7 %copy-start.4 = (s32[2]{0:T(128)S(1)}, s32[2]{0:T(128)}, u32[]{:S(2)}) copy-start(s32[2]{0:T(128)} %refs_0_.1) | copy-start | bytes 28
  5.4 4.3 %collective-permute-start.3 = (bf16[4,2,2,16,128]{4,3,2,1,0:T(8,128)(2,1)S(1)}, bf16[4,2,2,16,128]{4,3,2,1,0:T(8,128)(2,1)S(1)}, u32[]{:S(2)}, u32[]{:S(2)}) collective-permute-start(bf16[4,2,2,16,128]{4,3,2,1,0:T(8,128)(2,1)S(1)} %bitcast.13), channel_id=1, source_target_pairs={{0,4},{1,5},{4,0},{5,1},{8,12},{9,13},{12,8},{13,9},{2,6},{3,7},{6... | collective-permute-start | bytes 196616 | tf_op jit(solution)/shard_map/ppermute | solution.py:290
  7.1 0.8 %copy-start.2 = (bf16[2,2,64,64]{3,2,1,0:T(8,128)(2,1)S(1)}, bf16[2,2,64,64]{3,2,1,0:T(8,128)(2,1)}, u32[]{:S(2)}) copy-start(bf16[2,2,64,64]{3,2,1,0:T(8,128)(2,1)} %refs_4_.1) | copy-start | bytes 98308
  9.7 8.1 %collective-permute-start.4 = (bf16[6,2,2,16,128]{4,3,2,1,0:T(8,128)(2,1)S(1)}, bf16[6,2,2,16,128]{4,3,2,1,0:T(8,128)(2,1)S(1)}, u32[]{:S(2)}, u32[]{:S(2)}) collective-permute-start(bf16[6,2,2,16,128]{4,3,2,1,0:T(8,128)(2,1)S(1)} %join.1), channel_id=1, source_target_pairs={{0,1},{1,0},{2,3},{3,2},{4,5},{5,4},{6,7},{7,6},{8,9},{9,8},{10,11... | collective-permute-start | bytes 294920 | tf_op jit(solution)/shard_map/ppermute | solution.py:304
  9.8 5.8 %collective-permute-start.1 = (bf16[2,2,2,16,128]{4,3,2,1,0:T(8,128)(2,1)S(1)}, bf16[2,2,2,16,128]{4,3,2,1,0:T(8,128)(2,1)S(1)}, u32[]{:S(2)}, u32[]{:S(2)}) collective-permute-start(bf16[2,2,2,16,128]{4,3,2,1,0:T(8,128)(2,1)S(1)} %bitcast.17), channel_id=1, source_target_pairs={{0,12},{1,13},{4,8},{5,9},{8,4},{9,5},{12,0},{13,1},{2,14},{3,15},... | collective-permute-start | bytes 98312 | tf_op jit(solution)/shard_map/ppermute | solution.py:290
  12.6 5.2 %collective-permute-start.2 = (bf16[2,2,2,16,128]{4,3,2,1,0:T(8,128)(2,1)S(1)}, bf16[2,2,2,16,128]{4,3,2,1,0:T(8,128)(2,1)S(1)}, u32[]{:S(2)}, u32[]{:S(2)}) collective-permute-start(bf16[2,2,2,16,128]{4,3,2,1,0:T(8,128)(2,1)S(1)} %bitcast.16), channel_id=1, source_target_pairs={{0,13},{1,12},{4,9},{5,8},{8,5},{9,4},{12,1},{13,0},{2,15},{3,14},... | collective-permute-start | bytes 98312 | tf_op jit(solution)/shard_map/ppermute | solution.py:290
where the time goes:
time: 23.2 us; the launch traced here: 23 us
  starting transfers between devices  9.42 us (41%)
  Pallas kernels  7.3 us (31%)
  waiting for transfers between devices  4.33 us (19%)
  local copies, waits for them, and re-layouts  1.88 us (8%)
    ppermute x4, starting transfers between devices, shards(): arrived = lax.ppermute(chunk, ('az', 'acq'), straight)  9.35 us
    pallas_call x1, Pallas kernels, shards(): pl.pallas_call(body, out_shape=jax.ShapeDtypeStruct((blocks, columns, ele...  5.28 us
    ppermute x4, waiting for transfers between devices, shards(): arrived = lax.ppermute(chunk, ('az', 'acq'), straight)  4.33 us
    unnamed x12, local copies, waits for them, and re-layouts  1.8 us
    pallas_call x1, Pallas kernels, shards(): pl.pallas_call(lambda *refs: prepare_kernel(acq_share, pairwise, *refs),...  1.74 us
  transfers between devices with their start and end apart: 5, of which 2 were waited for; matrix products, arithmetic and copies ran while one was open for 0% of the time, Pallas kernels for 8%

commit v1 on v0

--- a/solution.py
+++ b/solution.py
@@ -14,8 +14,8 @@
 BF16 = jnp.bfloat16
 
 VMEM = pl.BlockSpec(memory_space=pltpu.VMEM)
-SMEM = pl.BlockSpec(memory_space=pltpu.SMEM)
 ANY = pl.BlockSpec(memory_space=pl.ANY)
+HBM = pl.BlockSpec(memory_space=pltpu.HBM)
 
 
 def dot(a, b, contract=(1, 0)):
@@ -24,27 +24,33 @@
     )
 
 
-def relay_kernel(places, x_ref, *refs):
-    chunks, sem = refs[:-1], refs[-1]
-    halves, acq_share = x_ref.shape[:2]
+def relay_kernel(places, extra, x_ref, *refs):
+    inputs, refs = refs[:extra], refs[extra:]
+    chunks, fetched = refs[: len(places)], refs[len(places) : len(places) + extra]
+    stack_ref, stack_sem, sems = refs[len(places) + extra :]
+    halves, acq_share, _, tiles = x_ref.shape[:4]
+    whole = pltpu.make_async_copy(x_ref, stack_ref, stack_sem)
+    whole.start()
+    copies = [
+        pltpu.make_async_copy(source, target, sems.at[at])
+        for at, (source, target) in enumerate(zip(inputs, fetched))
+    ]
+    for copy in copies:
+        copy.start()
     chip, core = lax.axis_index("az"), lax.axis_index("acq")
     cores = lax.axis_size("acq")
-    copies = []
+    whole.wait()
     for owners, chunk in zip(places, chunks):
         blocks = chunk.shape[0] // len(owners)
         for at, (d, j) in enumerate(owners):
             first = ((chip ^ d) * cores + (core ^ j)) * blocks
-            for half in range(halves):
-                for acq in range(acq_share):
-                    copies.append(
-                        pltpu.make_async_copy(
-                            x_ref.at[half, acq, pl.ds(first, blocks)],
-                            chunk.at[pl.ds(at * blocks, blocks), half, :, acq],
-                            sem,
-                        )
-                    )
-    for copy in copies:
-        copy.start()
+            for a in range(blocks):
+                for half in range(halves):
+                    for t in range(tiles):
+                        for acq in range(acq_share):
+                            chunk[at * blocks + a, half, t, acq] = stack_ref[
+                                half, acq, first + a, t
+                            ]
     for copy in copies:
         copy.wait()
 
@@ -53,43 +59,38 @@
     acq_share, relative, groups, counts, list_ref, steer_ref, filter_ref,
     first_ref, half_op_ref, op_t_ref, wiener_ref, select_ref, chosen_ref, clear_ref, fmat_ref,
 ):
-    acquisitions, _ = steer_ref.shape[2:]
-    blocks, columns = counts.shape
+    group_count, _, acquisitions, _ = steer_ref.shape
+    blocks, columns, per_block = list_ref.shape
     depth = 2 * acquisitions
     pixels = chosen_ref.shape[1]
-    entries = list_ref.shape[1]
-    per_block = entries // (blocks * columns)
-    lane = lax.broadcasted_iota(jnp.int32, (1, entries), 1)
-    limit = jnp.zeros((1, entries), jnp.int32)
+    first_group = lax.axis_index("rg") * group_count
+    row = lax.broadcasted_iota(jnp.int32, (per_block, per_block), 0)
+    lane = lax.broadcasted_iota(jnp.int32, (per_block, per_block), 1)
+    entry = lax.broadcasted_iota(jnp.int32, (per_block, pixels), 0)
+    pixel = lax.broadcasted_iota(jnp.int32, (per_block, pixels), 1)
     for a in range(blocks):
         for r in range(columns):
+            listed = list_ref[a, r : r + 1].astype(F32)
+            upright = jnp.sum(jnp.where(row == lane, listed, 0.0), axis=1, keepdims=True)
+            usable = entry < counts[a : a + 1, r : r + 1]
+            hit = (upright.astype(jnp.int32) == pixel) & usable
+            chosen = jnp.where(hit, 1.0, 0.0).astype(F32)
             start = (a * columns + r) * per_block
-            inside = (lane >= start) & (lane < start + per_block)
-            limit = jnp.where(inside, counts[a, r] + start, limit)
-    listed = jnp.where(lane < limit, list_ref[...], -1)
-    hits = lax.broadcasted_iota(jnp.int32, (pixels, entries), 0) == listed
-    chosen = jnp.transpose(jnp.where(hits, 1.0, 0.0).astype(F32))
-    chosen_ref[...] = chosen.astype(BF16)
-    for a in range(blocks):
-        for r in range(columns):
-            start = (a * columns + r) * per_block
-            covered = jnp.sum(chosen[start : start + per_block], axis=0, keepdims=True)
+            chosen_ref[start : start + per_block] = chosen.astype(BF16)
+            covered = jnp.sum(chosen, axis=0, keepdims=True)
             clear_ref[a * columns + r] = jnp.broadcast_to(1.0 - covered, clear_ref.shape[1:])
-    row = lax.broadcasted_iota(jnp.int32, (columns * depth, depth), 0)
-    column_at = lax.broadcasted_iota(jnp.int32, (columns * depth, depth), 1)
+    at = lax.broadcasted_iota(jnp.int32, (1, depth), 1)
+    half, acq = at // acquisitions, at % acquisitions
+    source = acq // acq_share
+    if relative:
+        cores = lax.axis_size("acq")
+        chip, core = lax.axis_index("az"), lax.axis_index("acq")
+        source = ((source // cores) ^ chip) * cores + ((source % cores) ^ core)
+    place = ((source * 2 + half) * acq_share + acq % acq_share) * columns
+    long = lax.broadcasted_iota(jnp.int32, (columns * depth, depth), 0)
     for r in range(columns):
-        g = groups[r] - lax.axis_index("rg") * steer_ref.shape[0]
-        pair = row // columns
-        acq = pair % acq_share
-        half = (pair // acq_share) % 2
-        source = pair // (2 * acq_share)
-        if relative:
-            cores = lax.axis_size("acq")
-            chip, core = lax.axis_index("az"), lax.axis_index("acq")
-            source = ((source // cores) ^ chip) * cores + ((source % cores) ^ core)
-        target = half * acquisitions + source * acq_share + acq
-        hit = (column_at == target) & (row % columns == r)
-        select = jnp.where(hit, 1.0, 0.0).astype(BF16)
+        g = jnp.max(groups[:, r : r + 1]) - first_group
+        select = jnp.where(long == place + r, 1.0, 0.0).astype(BF16)
         select_ref[r] = select
         real = steer_ref[g, 0]
         imag = steer_ref[g, 1]
@@ -109,8 +110,8 @@
         fmat_ref[:acquisitions, acquisitions:] = -filter_ref[g, 1].astype(F32)
         fmat_ref[acquisitions:, :acquisitions] = filter_ref[g, 1].astype(F32)
         fmat_ref[acquisitions:, acquisitions:] = filter_ref[g, 0].astype(F32)
-        beam = dot(op_t, fmat_ref[...].astype(BF16)).astype(BF16)
-        wiener_ref[r] = dot(beam, select, (1, 1)).astype(BF16)
+        spread = dot(fmat_ref[...].astype(BF16), select, (1, 1)).astype(BF16)
+        wiener_ref[r] = dot(op_t, spread).astype(BF16)
 
 
 def profile_body(
@@ -235,80 +236,78 @@
     rows = blocks * per_block
     tiles = pixels // LANES
     pairwise = acq_share * columns == 16 and cores == 2 and chips & (chips - 1) == 0
-    prepared = pl.pallas_call(
-        lambda *refs: prepare_kernel(acq_share, pairwise, *refs),
-        out_shape=[
-            jax.ShapeDtypeStruct((columns, columns * depth, 2 * elevation), BF16),
-            jax.ShapeDtypeStruct((columns, depth, 2 * elevation), BF16),
-            jax.ShapeDtypeStruct((columns, 2 * elevation, depth), BF16),
-            jax.ShapeDtypeStruct((columns, 2 * elevation, columns * depth), BF16),
-            jax.ShapeDtypeStruct((columns, columns * depth, depth), BF16),
-            jax.ShapeDtypeStruct((blocks * columns * per_block, pixels), BF16),
-            jax.ShapeDtypeStruct((blocks * columns, 8, pixels), F32),
-        ],
-        in_specs=[SMEM, SMEM, VMEM, VMEM, VMEM],
-        out_specs=[VMEM] * 7,
-        scratch_shapes=[pltpu.VMEM((depth, depth), F32)],
-        cost_estimate=pl.CostEstimate(
-            flops=1_000_000_000, bytes_accessed=4_000_000, transcendentals=0
-        ),
-        compiler_params=pltpu.CompilerParams(vmem_limit_bytes=16 << 20),
-        name="prepare",
-    )(range_group, lay_count, lay_list.reshape(1, -1), steering, wiener_filter)
+    small = [range_group.reshape(1, columns), lay_count, lay_list, steering, wiener_filter]
+
+    def prepare(small):
+        return pl.pallas_call(
+            lambda *refs: prepare_kernel(acq_share, pairwise, *refs),
+            out_shape=[
+                jax.ShapeDtypeStruct((columns, columns * depth, 2 * elevation), BF16),
+                jax.ShapeDtypeStruct((columns, depth, 2 * elevation), BF16),
+                jax.ShapeDtypeStruct((columns, 2 * elevation, depth), BF16),
+                jax.ShapeDtypeStruct((columns, 2 * elevation, columns * depth), BF16),
+                jax.ShapeDtypeStruct((columns, columns * depth, depth), BF16),
+                jax.ShapeDtypeStruct((blocks * columns * per_block, pixels), BF16),
+                jax.ShapeDtypeStruct((blocks * columns, 8, pixels), F32),
+            ],
+            in_specs=[VMEM] * len(small),
+            out_specs=[VMEM] * 7,
+            scratch_shapes=[pltpu.VMEM((depth, depth), F32)],
+            cost_estimate=pl.CostEstimate(
+                flops=1_000_000_000, bytes_accessed=4_000_000, transcendentals=0
+            ),
+            compiler_params=pltpu.CompilerParams(vmem_limit_bytes=16 << 20),
+            name="prepare",
+        )(*small)
 
     if pairwise:
         view = image_stack.reshape(halves, acq_share, azb_all, columns, tiles, LANES)
         view = view.transpose(0, 1, 2, 4, 3, 5)
-        far = chips - 1
         turns = sorted(range(1, chips), key=lambda d: (d < chips // 2, d))
-        places = [[(0, 0)], [(0, 1)]]
-        for d in turns:
-            places += [[(d, 0)], [(d, 1)]] if d == far else [[(d, 0), (d, 1)]]
+        places = [[(0, 0)], [(0, 1)]] + [[(d, 0), (d, 1)] for d in turns]
         unit = (halves, tiles, acq_share, columns, LANES)
-        chunks = pl.pallas_call(
-            lambda *refs: relay_kernel(places, *refs),
-            out_shape=[
-                jax.ShapeDtypeStruct((len(owners) * blocks,) + unit, BF16)
-                for owners in places
+        outputs = [
+            jax.ShapeDtypeStruct((len(owners) * blocks,) + unit, BF16) for owners in places
+        ]
+        relayed = pl.pallas_call(
+            lambda *refs: relay_kernel(places, len(small), *refs),
+            out_shape=outputs + [jax.ShapeDtypeStruct(x.shape, x.dtype) for x in small],
+            in_specs=[HBM] * (1 + len(small)),
+            out_specs=[VMEM] * (len(places) + len(small)),
+            scratch_shapes=[
+                pltpu.VMEM(view.shape, BF16),
+                pltpu.SemaphoreType.DMA,
+                pltpu.SemaphoreType.DMA((len(small),)),
             ],
-            in_specs=[ANY],
-            out_specs=[VMEM] * len(places),
-            scratch_shapes=[pltpu.SemaphoreType.DMA],
-            compiler_params=pltpu.CompilerParams(vmem_limit_bytes=2 << 20),
+            compiler_params=pltpu.CompilerParams(vmem_limit_bytes=4 << 20),
             name="relay",
-        )(view)
+        )(*[pltpu.with_memory_space_constraint(x, pltpu.HBM) for x in [view] + small])
+        prepared = prepare(relayed[len(places) :])
         flat = (halves, tiles, acq_share * columns, LANES)
-        chunks = [chunk.reshape((-1,) + flat) for chunk in chunks]
-        got, waiting = {(0, 0): chunks[0]}, [((0, 1), chunks[1])]
-        for owners, chunk in zip(places[2:], chunks[2:]):
-            d, j = owners[0]
-            straight = [
-                (c * cores + q, (c ^ d) * cores + (q ^ j))
-                for c in range(chips)
-                for q in range(cores)
-            ]
-            arrived = lax.ppermute(chunk, ("az", "acq"), straight)
-            got[d, j] = arrived
-            if len(owners) == 2:
-                waiting.append(((d, 1), arrived))
-        skips = [w.shape[0] - blocks for _, w in waiting]
+        chunks = [chunk.reshape((-1,) + flat) for chunk in relayed[: len(places)]]
+        got, waiting = {(0, 0): chunks[0]}, {(0, 1): chunks[1]}
+        for d, chunk in zip(turns, chunks[2:]):
+            arrived = lax.ppermute(chunk, "az", [(c, c ^ d) for c in range(chips)])
+            got[d, 0] = waiting[d, 1] = arrived
+        names = list(waiting)
+        skips = [waiting[n].shape[0] - blocks for n in names]
         passing = pl.pallas_call(
             lambda *refs: join_kernel(skips, *refs),
-            out_shape=jax.ShapeDtypeStruct((len(waiting) * blocks,) + flat, BF16),
-            in_specs=[VMEM] * len(waiting),
+            out_shape=jax.ShapeDtypeStruct((len(names) * blocks,) + flat, BF16),
+            in_specs=[VMEM] * len(names),
             out_specs=VMEM,
             compiler_params=pltpu.CompilerParams(vmem_limit_bytes=2 << 20),
             name="join",
-        )(*[w for _, w in waiting])
+        )(*[waiting[n] for n in names])
         passing, prepared = lax.optimization_barrier((passing, prepared))
         passed = lax.ppermute(passing, "acq", [(0, 1), (1, 0)])
         arrays, order = [], {}
         for place, array in got.items():
             order[place] = (len(arrays), ())
             arrays.append(array)
-        for at, (place, _) in enumerate(waiting):
+        for at, place in enumerate(names):
             order[place] = (len(arrays), (at,))
-        arrays.append(passed.reshape((len(waiting), blocks) + flat))
+        arrays.append(passed.reshape((len(names), blocks) + flat))
         order = [order[d, j] for d in range(chips) for j in range(cores)]
         lead = arrays
         body = lambda *refs: pieces_kernel(len(arrays), order, *refs)
@@ -319,6 +318,7 @@
         moved = moved.reshape(-1, acq_share, blocks, columns, pixels)
         lead = [moved.transpose(2, 0, 1, 3, 4).reshape(blocks, columns * depth, pixels)]
         body = plain_kernel
+        prepared = prepare(small)
 
     return pl.pallas_call(
         body,

time: 23.2 us -> 18.6 us (0.80)
  starting transfers between devices: 9.42 us -> 5.78 us
  local copies, waits for them, and re-layouts: 1.88 us -> 0 us
  waiting for transfers between devices: 4.33 us -> 4.94 us
  Pallas kernels: 7.3 us -> 7.73 us
    ppermute x4 -> x3, starting transfers between devices: 9.35 us -> 5.71 us  [shards(): arrived = lax.ppermute(chunk, 'az', [(c, c ^ d) for c in range(chips)])]
    unnamed x12 -> x0, local copies, waits for them, and re-layouts: 1.8 us -> none
    ppermute x1, waiting for transfers between devices: 0.01 us -> 1.33 us  [shards(): passed = lax.ppermute(passing, 'acq', [(0, 1), (1, 0)])]
    ppermute x4 -> x3, waiting for transfers between devices: 4.33 us -> 3.6 us  [shards(): arrived = lax.ppermute(chunk, 'az', [(c, c ^ d) for c in range(chips)])]
    pallas_call x2, Pallas kernels: 2.02 us -> 2.44 us  [the longest x1 1.32 us: shards(): pl.pallas_call(lambda *refs: relay_kernel(places, len(small), *refs), out...]
  transfers between devices with their start and end apart: 5 -> 4, of which waited for: 2 -> 4; matrix products, arithmetic and copies ran while one was open for 0% -> 0% of each run, Pallas kernels for 8% -> 6%
where the time goes in v1:
time: 18.6 us; the launch traced here: 18.5 us
  Pallas kernels  7.73 us (42%)
  starting transfers between devices  5.78 us (31%)
  waiting for transfers between devices  4.94 us (27%)
    ppermute x3, starting transfers between devices, shards(): arrived = lax.ppermute(chunk, 'az', [(c, c ^ d) for c in range(chips)])  5.71 us
    pallas_call x1, Pallas kernels, shards(): pl.pallas_call(body, out_shape=jax.ShapeDtypeStruct((blocks, columns, ele...  5.27 us
    ppermute x3, waiting for transfers between devices, shards(): arrived = lax.ppermute(chunk, 'az', [(c, c ^ d) for c in range(chips)])  3.6 us
    ppermute x1, waiting for transfers between devices, shards(): passed = lax.ppermute(passing, 'acq', [(0, 1), (1, 0)])  1.33 us
    pallas_call x1, Pallas kernels, shards(): pl.pallas_call(lambda *refs: relay_kernel(places, len(small), *refs), out...  1.32 us
    pallas_call x1, Pallas kernels, prepare(): pl.pallas_call(lambda *refs: prepare_kernel(acq_share, pairwise, *refs),...  1.12 us
  transfers between devices with their start and end apart: 4, of which 4 were waited for; matrix products, arithmetic and copies ran while one was open for 0% of the time, Pallas kernels for 6%

profile of v1, /device:TPU:0, one launch (start us, length us, event | category | flops | bytes accessed | tf_op | source)
XLA Modules:
  0.0 18.5 jit_solution(1002108974500646692)
XLA Ops:
  0.0 1.3 %relay.1 = (bf16[2,2,2,8,2,128]{5,4,3,2,1,0:T(2,128)(2,1)S(1)}, bf16[2,2,2,8,2,128]{5,4,3,2,1,0:T(2,128)(2,1)S(1)}, bf16[4,2,2,8,2,128]{5,4,3,2,1,0:T(2,128)(2,1...) custom-call(bf16[2,8,16,2,2,128]{5,4,3,2,1,0:T(2,128)(2,1)} %bitcast, ...), custom_call_target="tpu_custom_call" | custom-call | tf_op jit(solution)/shard_map/relay/pallas_call | solution.py:272
  1.3 4.1 %collective-permute-start = (bf16[4,2,2,16,128]{4,3,2,1,0:T(8,128)(2,1)S(1)}, bf16[4,2,2,16,128]{4,3,2,1,0:T(8,128)(2,1)S(1)}, u32[]{:S(2)}, u32[]{:S(2)}) collective-permute-start(bf16[4,2,2,16,128]{4,3,2,1,0:T(8,128)(2,1)S(1)} %bitcast.14), channel_id=1, source_target_pairs={{0,8},{4,12},{8,0},{12,4},{1,9},{5,13},{9,1},{13,5},{2,10},{6,14},... | collective-permute-start | bytes 196616 | tf_op jit(solution)/shard_map/ppermute | solution.py:290
  5.5 1.3 %collective-permute-start.1 = (bf16[4,2,2,16,128]{4,3,2,1,0:T(8,128)(2,1)S(1)}, bf16[4,2,2,16,128]{4,3,2,1,0:T(8,128)(2,1)S(1)}, u32[]{:S(2)}, u32[]{:S(2)}) collective-permute-start(bf16[4,2,2,16,128]{4,3,2,1,0:T(8,128)(2,1)S(1)} %bitcast.13), channel_id=1, source_target_pairs={{0,12},{4,8},{8,4},{12,0},{1,13},{5,9},{9,5},{13,1},{2,14},{6,10},... | collective-permute-start | bytes 196616 | tf_op jit(solution)/shard_map/ppermute | solution.py:290
  6.8 0.2 %collective-permute-start.2 = (bf16[4,2,2,16,128]{4,3,2,1,0:T(8,128)(2,1)S(1)}, bf16[4,2,2,16,128]{4,3,2,1,0:T(8,128)(2,1)S(1)}, u32[]{:S(2)}, u32[]{:S(2)}) collective-permute-start(bf16[4,2,2,16,128]{4,3,2,1,0:T(8,128)(2,1)S(1)} %bitcast.12), channel_id=1, source_target_pairs={{0,4},{4,0},{8,12},{12,8},{1,5},{5,1},{9,13},{13,9},{2,6},{6,2},{1... | collective-permute-start | bytes 196616 | tf_op jit(solution)/shard_map/ppermute | solution.py:290
  7.0 1.1 %prepare.1 = (bf16[2,256,1024]{2,1,0:T(8,128)(2,1)S(1)}, bf16[2,128,1024]{2,1,0:T(8,128)(2,1)S(1)}, bf16[2,1024,128]{2,1,0:T(8,128)(2,1)S(1)}, bf16[2,1024,256]{...) custom-call(s32[1,2]{1,0:T(1,128)S(1)} %get-tuple-element.35.refs_0_, ...), custom_call_target="tpu_custom_call" | custom-call | flops 1000000000 | bytes 4000000 | tf_op jit(solution)/shard_map/prepare/pallas_call | solution.py:242
  8.2 1.0 %collective-permute-done.refs_1_ = bf16[4,2,2,16,128]{4,3,2,1,0:T(8,128)(2,1)S(1)} collective-permute-done((bf16[4,2,2,16,128]{4,3,2,1,0:T(8,128)(2,1)S(1)}, bf16[4,2,2,16,128]{4,3,2,1,0:T(8,128)(2,1)S(1)}, u32[]{:S(2)}, u32[]{:S(2)}) %collective-permute-start) | collective-permute-done | bytes 65568 | tf_op jit(solution)/shard_map/ppermute | solution.py:290
  9.2 2.5 %collective-permute-done.1.refs_2_ = bf16[4,2,2,16,128]{4,3,2,1,0:T(8,128)(2,1)S(1)} collective-permute-done((bf16[4,2,2,16,128]{4,3,2,1,0:T(8,128)(2,1)S(1)}, bf16[4,2,2,16,128]{4,3,2,1,0:T(8,128)(2,1)S(1)}, u32[]{:S(2)}, u32[]{:S(2)}) %collective-permute-start.1) | collective-permute-done | bytes 65568 | tf_op jit(solution)/shard_map/ppermute | solution.py:290
  11.6 0.1 collective-permute-done.2.refs_3_
  11.8 0.1 collective-permute-start.3
  11.9 1.3 %collective-permute-done.3 = bf16[8,2,2,16,128]{4,3,2,1,0:T(8,128)(2,1)S(1)} collective-permute-done((bf16[8,2,2,16,128]{4,3,2,1,0:T(8,128)(2,1)S(1)}, bf16[8,2,2,16,128]{4,3,2,1,0:T(8,128)(2,1)S(1)}, u32[]{:S(2)}, u32[]{:S(2)}) %collective-permute-start.3) | collective-permute-done | bytes 131104 | tf_op jit(solution)/shard_map/ppermute | solution.py:303
  13.2 5.3 %profiles.1 = bf16[2,2,512,256]{3,2,1,0:T(8,128)(2,1)} custom-call(bf16[2,2,2,16,128]{4,3,2,1,0:T(8,128)(2,1)S(1)} %bitcast.15, bf16[4,2,2,16,128]{4,3,2,1,0:T(8,128)(2,1)S(1)} %collective-permute-done.refs_1_, bf16[4,2,2,16,128]{4,3,2,1,0:T(8,128)(2,1)S(1)} %collective-permute-done.1.refs_2_, ...), custom_call_target="tpu_custom_call" | custom-call | flops 2000000000 | bytes 4000000 | tf_op jit(solution)/shard_map/profiles/pallas_call | solution.py:323
  (1 shorter events, 0.0 us)
Async XLA Ops:
  1.3 7.8 %collective-permute-start = (bf16[4,2,2,16,128]{4,3,2,1,0:T(8,128)(2,1)S(1)}, bf16[4,2,2,16,128]{4,3,2,1,0:T(8,128)(2,1)S(1)}, u32[]{:S(2)}, u32[]{:S(2)}) collective-permute-start(bf16[4,2,2,16,128]{4,3,2,1,0:T(8,128)(2,1)S(1)} %bitcast.14), channel_id=1, source_target_pairs={{0,8},{4,12},{8,0},{12,4},{1,9},{5,13},{9,1},{13,5},{2,10},{6,14},... | collective-permute-start | bytes 196616 | tf_op jit(solution)/shard_map/ppermute | solution.py:290
  5.5 6.2 %collective-permute-start.1 = (bf16[4,2,2,16,128]{4,3,2,1,0:T(8,128)(2,1)S(1)}, bf16[4,2,2,16,128]{4,3,2,1,0:T(8,128)(2,1)S(1)}, u32[]{:S(2)}, u32[]{:S(2)}) collective-permute-start(bf16[4,2,2,16,128]{4,3,2,1,0:T(8,128)(2,1)S(1)} %bitcast.13), channel_id=1, source_target_pairs={{0,12},{4,8},{8,4},{12,0},{1,13},{5,9},{9,5},{13,1},{2,14},{6,10},... | collective-permute-start | bytes 196616 | tf_op jit(solution)/shard_map/ppermute | solution.py:290
  6.8 5.0 %collective-permute-start.2 = (bf16[4,2,2,16,128]{4,3,2,1,0:T(8,128)(2,1)S(1)}, bf16[4,2,2,16,128]{4,3,2,1,0:T(8,128)(2,1)S(1)}, u32[]{:S(2)}, u32[]{:S(2)}) collective-permute-start(bf16[4,2,2,16,128]{4,3,2,1,0:T(8,128)(2,1)S(1)} %bitcast.12), channel_id=1, source_target_pairs={{0,4},{4,0},{8,12},{12,8},{1,5},{5,1},{9,13},{13,9},{2,6},{6,2},{1... | collective-permute-start | bytes 196616 | tf_op jit(solution)/shard_map/ppermute | solution.py:290
  11.8 1.4 %collective-permute-start.3 = (bf16[8,2,2,16,128]{4,3,2,1,0:T(8,128)(2,1)S(1)}, bf16[8,2,2,16,128]{4,3,2,1,0:T(8,128)(2,1)S(1)}, u32[]{:S(2)}, u32[]{:S(2)}) collective-permute-start(bf16[8,2,2,16,128]{4,3,2,1,0:T(8,128)(2,1)S(1)} %join.1), channel_id=1, source_target_pairs={{0,1},{1,0},{2,3},{3,2},{4,5},{5,4},{6,7},{7,6},{8,9},{9,8},{10,11... | collective-permute-start | bytes 393224 | tf_op jit(solution)/shard_map/ppermute | solution.py:303

commit v2 on v1

--- a/solution.py
+++ b/solution.py
@@ -9,7 +9,6 @@
 STEP_SIZE = 0.5
 SHRINK = 0.25
 LANES = 128
-WIENER_ROWS = 128
 F32 = jnp.float32
 BF16 = jnp.bfloat16
 
@@ -59,10 +58,10 @@
     acq_share, relative, groups, counts, list_ref, steer_ref, filter_ref,
     first_ref, half_op_ref, op_t_ref, wiener_ref, select_ref, chosen_ref, clear_ref, fmat_ref,
 ):
-    group_count, _, acquisitions, _ = steer_ref.shape
+    group_count, _, acquisitions, elevation = steer_ref.shape
     blocks, columns, per_block = list_ref.shape
     depth = 2 * acquisitions
-    pixels = chosen_ref.shape[1]
+    pixels = chosen_ref.shape[0] * LANES
     first_group = lax.axis_index("rg") * group_count
     row = lax.broadcasted_iota(jnp.int32, (per_block, per_block), 0)
     lane = lax.broadcasted_iota(jnp.int32, (per_block, per_block), 1)
@@ -76,7 +75,9 @@
             hit = (upright.astype(jnp.int32) == pixel) & usable
             chosen = jnp.where(hit, 1.0, 0.0).astype(F32)
             start = (a * columns + r) * per_block
-            chosen_ref[start : start + per_block] = chosen.astype(BF16)
+            for t in range(pixels // LANES):
+                part = chosen[:, t * LANES : (t + 1) * LANES]
+                chosen_ref[t, start : start + per_block] = part.astype(BF16)
             covered = jnp.sum(chosen, axis=0, keepdims=True)
             clear_ref[a * columns + r] = jnp.broadcast_to(1.0 - covered, clear_ref.shape[1:])
     at = lax.broadcasted_iota(jnp.int32, (1, depth), 1)
@@ -94,24 +95,31 @@
         select_ref[r] = select
         real = steer_ref[g, 0]
         imag = steer_ref[g, 1]
-        operator = jnp.concatenate(
-            [
-                jnp.concatenate([real, -imag], axis=1),
-                jnp.concatenate([imag, real], axis=1),
-            ],
-            axis=0,
-        )
+        slabs = []
+        for at in range(0, elevation, LANES):
+            re, im = real[:, at : at + LANES], imag[:, at : at + LANES]
+            slabs += [jnp.concatenate([re, im], axis=0), jnp.concatenate([-im, re], axis=0)]
+        operator = jnp.concatenate(slabs, axis=1)
         half_op = operator * jnp.asarray(STEP_SIZE, BF16)
-        half_op_ref[r] = half_op
-        first_ref[r] = dot(select, half_op).astype(BF16)
+        first = dot(select, half_op).astype(BF16)
         op_t = jnp.transpose(operator.astype(F32)).astype(BF16)
-        op_t_ref[r] = op_t
+        for slab in range(op_t_ref.shape[1]):
+            op_t_ref[r, slab] = op_t[slab * 2 * LANES : (slab + 1) * 2 * LANES]
+        for slab in range(len(slabs)):
+            half_op_ref[r, slab] = half_op[:, slab * LANES : (slab + 1) * LANES]
+            first_ref[r, slab] = first[:, slab * LANES : (slab + 1) * LANES]
         fmat_ref[:acquisitions, :acquisitions] = filter_ref[g, 0].astype(F32)
         fmat_ref[:acquisitions, acquisitions:] = -filter_ref[g, 1].astype(F32)
         fmat_ref[acquisitions:, :acquisitions] = filter_ref[g, 1].astype(F32)
         fmat_ref[acquisitions:, acquisitions:] = filter_ref[g, 0].astype(F32)
         spread = dot(fmat_ref[...].astype(BF16), select, (1, 1)).astype(BF16)
-        wiener_ref[r] = dot(op_t, spread).astype(BF16)
+        wiener = dot(op_t, spread).astype(BF16)
+        for slab in range(wiener_ref.shape[1]):
+            wiener_ref[r, slab] = wiener[:, slab * LANES : (slab + 1) * LANES]
+
+
+def wide(ref, *at):
+    return jnp.concatenate([ref[where] for where in at], axis=-1)
 
 
 def profile_body(
@@ -119,14 +127,16 @@
     out_ref, real_ref, imag_ref, rounded_ref, target_ref, image_ref, sem,
 ):
     blocks, columns, elevation, _ = out_ref.shape
-    per_block = chosen_ref.shape[0] // (blocks * columns)
+    tiles, entries = chosen_ref.shape[:2]
+    per_block = entries // (blocks * columns)
+    slabs = elevation // LANES
+
+    def chosen(first, size):
+        return wide(chosen_ref, *[(t, slice(first, first + size)) for t in range(tiles)])
+
+    share = columns * per_block
     picked = [
-        dot(
-            chosen_ref[a * columns * per_block : (a + 1) * columns * per_block],
-            grid(a),
-            (1, 1),
-        ).astype(BF16)
-        for a in range(blocks)
+        dot(chosen(a * share, share), grid(a), (1, 1)).astype(BF16) for a in range(blocks)
     ]
     picked = [
         jnp.concatenate([p[r * per_block : (r + 1) * per_block] for p in picked], axis=0)
@@ -135,61 +145,96 @@
     for r in range(columns):
         target_ref[r] = dot(picked[r], select_ref[r])
 
-    tile = 256
+    def predicted(r):
+        size = rounded_ref.shape[2]
+        deep = op_t_ref.shape[2] // LANES
+        total = None
+        for at in range(0, op_t_ref.shape[1], 2):
+            stacked = jnp.concatenate(
+                [
+                    wide(rounded_ref, *[(r, (at + j) * deep + k) for k in range(deep)])
+                    for j in range(2)
+                ],
+                axis=0,
+            )
+            both = dot(stacked, wide(op_t_ref, (r, at), (r, at + 1)))
+            total = both if total is None else total + both
+        depth = op_t_ref.shape[3]
+        return total[:size, :depth] + total[size:, depth:]
 
     def update(r, misfit, op_ref, first):
-        for at in range(0, elevation, tile):
-            zr = dot(misfit, op_ref[r, :, at : at + tile])
-            zi = dot(misfit, op_ref[r, :, elevation + at : elevation + at + tile])
+        for slab in range(slabs):
+            z = dot(misfit, wide(op_ref, (r, 2 * slab), (r, 2 * slab + 1)))
+            zr, zi = z[:, :LANES], z[:, LANES:]
             if not first:
-                zr = zr + real_ref[r, :, at : at + tile]
-                zi = zi + imag_ref[r, :, at : at + tile]
+                zr = zr + real_ref[r, slab]
+                zi = zi + imag_ref[r, slab]
             magnitude = zr * zr + zi * zi
             factor = jnp.maximum(
                 1.0 - SHRINK * lax.rsqrt(jnp.maximum(magnitude, SHRINK * SHRINK)), 0.0
             )
             xr = zr * factor
             xi = zi * factor
-            real_ref[r, :, at : at + tile] = xr
-            imag_ref[r, :, at : at + tile] = xi
-            rounded_ref[r, :, at : at + tile] = xr.astype(BF16)
-            rounded_ref[r, :, elevation + at : elevation + at + tile] = xi.astype(BF16)
-
-    shares = [(a, r, at) for a in range(blocks) for at in range(0, elevation, WIENER_ROWS)
-              for r in range(columns)]
-
-    def wiener(a, r, at):
-        br = dot(wiener_ref[r, at : at + WIENER_ROWS], grid(a))
-        bi = dot(wiener_ref[r, elevation + at : elevation + at + WIENER_ROWS], grid(a))
+            real_ref[r, slab] = xr
+            imag_ref[r, slab] = xi
+            rounded_ref[r, 2 * slab] = xr.astype(BF16)
+            rounded_ref[r, 2 * slab + 1] = xi.astype(BF16)
+
+    shares = [
+        (a, r, slab) for a in range(blocks) for slab in range(slabs) for r in range(columns)
+    ]
+
+    def wiener(a, r, slab):
+        first = 2 * slab * LANES
+        depths = range(wiener_ref.shape[1])
+        br = dot(wide(wiener_ref, *[(r, k, slice(first, first + LANES)) for k in depths]), grid(a))
+        first += LANES
+        bi = dot(wide(wiener_ref, *[(r, k, slice(first, first + LANES)) for k in depths]), grid(a))
         power = (br * br + bi * bi) * clear_ref[a * columns + r, :1]
-        image_ref[a, r, at : at + WIENER_ROWS] = power.astype(BF16)
-
-    done = 0
+        power = power.astype(BF16)
+        image_ref[a, r, slab * LANES : (slab + 1) * LANES] = power
+
+    todo = list(shares)
+
+    def more(count):
+        for part in todo[:count]:
+            wiener(*part)
+        del todo[:count]
+
+    each = len(shares) // ITERS
     for t in range(ITERS):
+        if t == 0:
+            misfits = picked
+        else:
+            misfits = [(target_ref[r] - predicted(r)).astype(BF16) for r in range(columns)]
         for r in range(columns):
-            if t == 0:
-                update(r, picked[r], first_ref, True)
-            else:
-                misfit = (target_ref[r] - dot(rounded_ref[r], op_t_ref[r])).astype(BF16)
-                update(r, misfit, half_op_ref, False)
-        until = len(shares) * (t + 1) // ITERS
-        for share in shares[done:until]:
-            wiener(*share)
-        done = until
+            update(r, misfits[r], half_op_ref if t else first_ref, t == 0)
+            more(each // columns)
+
+    def copies(a, r, slab):
+        where = pl.ds(slab * LANES, LANES)
+        return [
+            pltpu.make_async_copy(image_ref.at[a, r, where], out_ref.at[a, r, where], sem)
+        ]
 
     for r in range(columns):
         for a in range(blocks):
-            start = (a * columns + r) * per_block
-            chosen = chosen_ref[start : start + per_block]
-            xr = real_ref[r, a * per_block : (a + 1) * per_block]
-            xi = imag_ref[r, a * per_block : (a + 1) * per_block]
-            strength = (xr * xr + xi * xi).astype(BF16)
-            placed = dot(strength, chosen, (0, 0)).astype(BF16)
-            image_ref[a, r] = image_ref[a, r] + placed
-            pltpu.make_async_copy(image_ref.at[a, r], out_ref.at[a, r], sem).start()
+            rows = slice(a * per_block, (a + 1) * per_block)
+            for slab in range(slabs):
+                xr, xi = real_ref[r, slab, rows], imag_ref[r, slab, rows]
+                strength = (xr * xr + xi * xi).astype(BF16)
+                placed = dot(
+                    strength, chosen((a * columns + r) * per_block, per_block), (0, 0)
+                ).astype(BF16)
+                where = slice(slab * LANES, (slab + 1) * LANES)
+                image_ref[a, r, where] = image_ref[a, r, where] + placed
+                for copy in copies(a, r, slab):
+                    copy.start()
     for a in range(blocks):
         for r in range(columns):
-            pltpu.make_async_copy(image_ref.at[a, r], out_ref.at[a, r], sem).wait()
+            for slab in range(slabs):
+                for copy in copies(a, r, slab):
+                    copy.wait()
 
 
 def join_kernel(skips, *refs):
@@ -235,6 +280,7 @@
     per_block = lay_list.shape[2]
     rows = blocks * per_block
     tiles = pixels // LANES
+    slabs = 2 * elevation // LANES
     pairwise = acq_share * columns == 16 and cores == 2 and chips & (chips - 1) == 0
     small = [range_group.reshape(1, columns), lay_count, lay_list, steering, wiener_filter]
 
@@ -242,12 +288,14 @@
         return pl.pallas_call(
             lambda *refs: prepare_kernel(acq_share, pairwise, *refs),
             out_shape=[
-                jax.ShapeDtypeStruct((columns, columns * depth, 2 * elevation), BF16),
-                jax.ShapeDtypeStruct((columns, depth, 2 * elevation), BF16),
-                jax.ShapeDtypeStruct((columns, 2 * elevation, depth), BF16),
-                jax.ShapeDtypeStruct((columns, 2 * elevation, columns * depth), BF16),
+                jax.ShapeDtypeStruct((columns, slabs, columns * depth, LANES), BF16),
+                jax.ShapeDtypeStruct((columns, slabs, depth, LANES), BF16),
+                jax.ShapeDtypeStruct((columns, slabs // 2, 2 * LANES, depth), BF16),
+                jax.ShapeDtypeStruct(
+                    (columns, columns * depth // LANES, 2 * elevation, LANES), BF16
+                ),
                 jax.ShapeDtypeStruct((columns, columns * depth, depth), BF16),
-                jax.ShapeDtypeStruct((blocks * columns * per_block, pixels), BF16),
+                jax.ShapeDtypeStruct((tiles, blocks * columns * per_block, LANES), BF16),
                 jax.ShapeDtypeStruct((blocks * columns, 8, pixels), F32),
             ],
             in_specs=[VMEM] * len(small),
@@ -326,9 +374,9 @@
         in_specs=[VMEM] * (len(lead) + len(prepared)),
         out_specs=ANY,
         scratch_shapes=[
-            pltpu.VMEM((columns, rows, elevation), F32),
-            pltpu.VMEM((columns, rows, elevation), F32),
-            pltpu.VMEM((columns, rows, 2 * elevation), BF16),
+            pltpu.VMEM((columns, slabs // 2, rows, LANES), F32),
+            pltpu.VMEM((columns, slabs // 2, rows, LANES), F32),
+            pltpu.VMEM((columns, slabs, rows, LANES), BF16),
             pltpu.VMEM((columns, rows, depth), F32),
             pltpu.VMEM((blocks, columns, elevation, pixels), BF16),
             pltpu.SemaphoreType.DMA,

time: 18.6 us -> 17.8 us (0.957)
  Pallas kernels: 7.73 us -> 6.92 us
    pallas_call x1, Pallas kernels: 5.27 us -> 4.45 us  [shards(): pl.pallas_call(body, out_shape=jax.ShapeDtypeStruct((blocks, columns, ele...]
  transfers between devices with their start and end apart: 4 -> 4, of which waited for: 4 -> 4; matrix products, arithmetic and copies ran while one was open for 0% -> 0% of each run, Pallas kernels for 6% -> 7%
where the time goes in v2:
time: 17.8 us; the launch traced here: 17.6 us
  Pallas kernels  6.92 us (39%)
  starting transfers between devices  5.78 us (32%)
  waiting for transfers between devices  4.92 us (28%)
    ppermute x3, starting transfers between devices, shards(): arrived = lax.ppermute(chunk, 'az', [(c, c ^ d) for c in range(chips)])  5.71 us
    pallas_call x1, Pallas kernels, shards(): pl.pallas_call(body, out_shape=jax.ShapeDtypeStruct((blocks, columns, ele...  4.45 us
    ppermute x3, waiting for transfers between devices, shards(): arrived = lax.ppermute(chunk, 'az', [(c, c ^ d) for c in range(chips)])  3.58 us
    ppermute x1, waiting for transfers between devices, shards(): passed = lax.ppermute(passing, 'acq', [(0, 1), (1, 0)])  1.33 us
    pallas_call x1, Pallas kernels, shards(): pl.pallas_call(lambda *refs: relay_kernel(places, len(small), *refs), out...  1.32 us
    pallas_call x1, Pallas kernels, prepare(): pl.pallas_call(lambda *refs: prepare_kernel(acq_share, pairwise, *refs),...  1.14 us
  transfers between devices with their start and end apart: 4, of which 4 were waited for; matrix products, arithmetic and copies ran while one was open for 0% of the time, Pallas kernels for 7%

profile of v2, /device:TPU:0, one launch (start us, length us, event | category | flops | bytes accessed | tf_op | source)
XLA Modules:
  0.0 17.6 jit_solution(13837829646746337359)
XLA Ops:
  0.0 1.3 %relay.1 = (bf16[2,2,2,8,2,128]{5,4,3,2,1,0:T(2,128)(2,1)S(1)}, bf16[2,2,2,8,2,128]{5,4,3,2,1,0:T(2,128)(2,1)S(1)}, bf16[4,2,2,8,2,128]{5,4,3,2,1,0:T(2,128)(2,1...) custom-call(bf16[2,8,16,2,2,128]{5,4,3,2,1,0:T(2,128)(2,1)} %bitcast, ...), custom_call_target="tpu_custom_call" | custom-call | tf_op jit(solution)/shard_map/relay/pallas_call | solution.py:320
  1.3 4.1 %collective-permute-start = (bf16[4,2,2,16,128]{4,3,2,1,0:T(8,128)(2,1)S(1)}, bf16[4,2,2,16,128]{4,3,2,1,0:T(8,128)(2,1)S(1)}, u32[]{:S(2)}, u32[]{:S(2)}) collective-permute-start(bf16[4,2,2,16,128]{4,3,2,1,0:T(8,128)(2,1)S(1)} %bitcast.14), channel_id=1, source_target_pairs={{0,8},{4,12},{8,0},{12,4},{1,9},{5,13},{9,1},{13,5},{2,10},{6,14},... | collective-permute-start | bytes 196616 | tf_op jit(solution)/shard_map/ppermute | solution.py:338
  5.5 1.3 %collective-permute-start.1 = (bf16[4,2,2,16,128]{4,3,2,1,0:T(8,128)(2,1)S(1)}, bf16[4,2,2,16,128]{4,3,2,1,0:T(8,128)(2,1)S(1)}, u32[]{:S(2)}, u32[]{:S(2)}) collective-permute-start(bf16[4,2,2,16,128]{4,3,2,1,0:T(8,128)(2,1)S(1)} %bitcast.13), channel_id=1, source_target_pairs={{0,12},{4,8},{8,4},{12,0},{1,13},{5,9},{9,5},{13,1},{2,14},{6,10},... | collective-permute-start | bytes 196616 | tf_op jit(solution)/shard_map/ppermute | solution.py:338
  6.8 0.2 %collective-permute-start.2 = (bf16[4,2,2,16,128]{4,3,2,1,0:T(8,128)(2,1)S(1)}, bf16[4,2,2,16,128]{4,3,2,1,0:T(8,128)(2,1)S(1)}, u32[]{:S(2)}, u32[]{:S(2)}) collective-permute-start(bf16[4,2,2,16,128]{4,3,2,1,0:T(8,128)(2,1)S(1)} %bitcast.12), channel_id=1, source_target_pairs={{0,4},{4,0},{8,12},{12,8},{1,5},{5,1},{9,13},{13,9},{2,6},{6,2},{1... | collective-permute-start | bytes 196616 | tf_op jit(solution)/shard_map/ppermute | solution.py:338
  7.0 1.1 %prepare.1 = (bf16[2,8,256,128]{3,2,1,0:T(8,128)(2,1)S(1)}, bf16[2,8,128,128]{3,2,1,0:T(8,128)(2,1)S(1)}, bf16[2,4,256,128]{3,2,1,0:T(8,128)(2,1)S(1)}, bf16[2,2...) custom-call(s32[1,2]{1,0:T(1,128)S(1)} %get-tuple-element.35.refs_0_, ...), custom_call_target="tpu_custom_call" | custom-call | flops 1000000000 | bytes 4000000 | tf_op jit(solution)/shard_map/prepare/pallas_call | solution.py:288
  8.2 1.0 %collective-permute-done.refs_1_ = bf16[4,2,2,16,128]{4,3,2,1,0:T(8,128)(2,1)S(1)} collective-permute-done((bf16[4,2,2,16,128]{4,3,2,1,0:T(8,128)(2,1)S(1)}, bf16[4,2,2,16,128]{4,3,2,1,0:T(8,128)(2,1)S(1)}, u32[]{:S(2)}, u32[]{:S(2)}) %collective-permute-start) | collective-permute-done | bytes 65568 | tf_op jit(solution)/shard_map/ppermute | solution.py:338
  9.2 2.5 %collective-permute-done.1.refs_2_ = bf16[4,2,2,16,128]{4,3,2,1,0:T(8,128)(2,1)S(1)} collective-permute-done((bf16[4,2,2,16,128]{4,3,2,1,0:T(8,128)(2,1)S(1)}, bf16[4,2,2,16,128]{4,3,2,1,0:T(8,128)(2,1)S(1)}, u32[]{:S(2)}, u32[]{:S(2)}) %collective-permute-start.1) | collective-permute-done | bytes 65568 | tf_op jit(solution)/shard_map/ppermute | solution.py:338
  11.6 0.1 collective-permute-done.2.refs_3_
  11.8 0.1 collective-permute-start.3
  11.9 1.3 %collective-permute-done.3 = bf16[8,2,2,16,128]{4,3,2,1,0:T(8,128)(2,1)S(1)} collective-permute-done((bf16[8,2,2,16,128]{4,3,2,1,0:T(8,128)(2,1)S(1)}, bf16[8,2,2,16,128]{4,3,2,1,0:T(8,128)(2,1)S(1)}, u32[]{:S(2)}, u32[]{:S(2)}) %collective-permute-start.3) | collective-permute-done | bytes 131104 | tf_op jit(solution)/shard_map/ppermute | solution.py:351
  13.2 4.4 %profiles.1 = bf16[2,2,512,256]{3,2,1,0:T(8,128)(2,1)} custom-call(bf16[2,2,2,16,128]{4,3,2,1,0:T(8,128)(2,1)S(1)} %bitcast.15, bf16[4,2,2,16,128]{4,3,2,1,0:T(8,128)(2,1)S(1)} %collective-permute-done.refs_1_, bf16[4,2,2,16,128]{4,3,2,1,0:T(8,128)(2,1)S(1)} %collective-permute-done.1.refs_2_, ...), custom_call_target="tpu_custom_call" | custom-call | flops 2000000000 | bytes 4000000 | tf_op jit(solution)/shard_map/profiles/pallas_call | solution.py:371
  (1 shorter events, 0.0 us)
Async XLA Ops:
  1.3 7.8 %collective-permute-start = (bf16[4,2,2,16,128]{4,3,2,1,0:T(8,128)(2,1)S(1)}, bf16[4,2,2,16,128]{4,3,2,1,0:T(8,128)(2,1)S(1)}, u32[]{:S(2)}, u32[]{:S(2)}) collective-permute-start(bf16[4,2,2,16,128]{4,3,2,1,0:T(8,128)(2,1)S(1)} %bitcast.14), channel_id=1, source_target_pairs={{0,8},{4,12},{8,0},{12,4},{1,9},{5,13},{9,1},{13,5},{2,10},{6,14},... | collective-permute-start | bytes 196616 | tf_op jit(solution)/shard_map/ppermute | solution.py:338
  5.5 6.2 %collective-permute-start.1 = (bf16[4,2,2,16,128]{4,3,2,1,0:T(8,128)(2,1)S(1)}, bf16[4,2,2,16,128]{4,3,2,1,0:T(8,128)(2,1)S(1)}, u32[]{:S(2)}, u32[]{:S(2)}) collective-permute-start(bf16[4,2,2,16,128]{4,3,2,1,0:T(8,128)(2,1)S(1)} %bitcast.13), channel_id=1, source_target_pairs={{0,12},{4,8},{8,4},{12,0},{1,13},{5,9},{9,5},{13,1},{2,14},{6,10},... | collective-permute-start | bytes 196616 | tf_op jit(solution)/shard_map/ppermute | solution.py:338
  6.8 5.0 %collective-permute-start.2 = (bf16[4,2,2,16,128]{4,3,2,1,0:T(8,128)(2,1)S(1)}, bf16[4,2,2,16,128]{4,3,2,1,0:T(8,128)(2,1)S(1)}, u32[]{:S(2)}, u32[]{:S(2)}) collective-permute-start(bf16[4,2,2,16,128]{4,3,2,1,0:T(8,128)(2,1)S(1)} %bitcast.12), channel_id=1, source_target_pairs={{0,4},{4,0},{8,12},{12,8},{1,5},{5,1},{9,13},{13,9},{2,6},{6,2},{1... | collective-permute-start | bytes 196616 | tf_op jit(solution)/shard_map/ppermute | solution.py:338
  11.8 1.4 %collective-permute-start.3 = (bf16[8,2,2,16,128]{4,3,2,1,0:T(8,128)(2,1)S(1)}, bf16[8,2,2,16,128]{4,3,2,1,0:T(8,128)(2,1)S(1)}, u32[]{:S(2)}, u32[]{:S(2)}) collective-permute-start(bf16[8,2,2,16,128]{4,3,2,1,0:T(8,128)(2,1)S(1)} %join.1), channel_id=1, source_target_pairs={{0,1},{1,0},{2,3},{3,2},{4,5},{5,4},{6,7},{7,6},{8,9},{9,8},{10,11... | collective-permute-start | bytes 393224 | tf_op jit(solution)/shard_map/ppermute | solution.py:351

commit v3 on v2

--- a/solution.py
+++ b/solution.py
@@ -23,26 +23,34 @@
     )
 
 
-def relay_kernel(places, extra, x_ref, *refs):
-    inputs, refs = refs[:extra], refs[extra:]
-    chunks, fetched = refs[: len(places)], refs[len(places) : len(places) + extra]
-    stack_ref, stack_sem, sems = refs[len(places) + extra :]
-    halves, acq_share, _, tiles = x_ref.shape[:4]
-    whole = pltpu.make_async_copy(x_ref, stack_ref, stack_sem)
+def turns_of(chips):
+    if chips == 4:
+        return [[1, 3, 0, 2], [3, 2, 1, 0], [2, 0, 3, 1]]
+    far = sorted(range(1, chips), key=lambda d: (d < chips // 2, d))
+    return [[c ^ d for c in range(chips)] for d in far]
+
+
+def pick(table, index):
+    return sum(jnp.where(index == at, value, 0) for at, value in enumerate(table))
+
+
+def relay_kernel(places, x_ref, *refs):
+    chunks, stack_ref, sem = refs[:-2], refs[-2], refs[-1]
+    whole = pltpu.make_async_copy(x_ref, stack_ref, sem)
     whole.start()
-    copies = [
-        pltpu.make_async_copy(source, target, sems.at[at])
-        for at, (source, target) in enumerate(zip(inputs, fetched))
-    ]
-    for copy in copies:
-        copy.start()
     chip, core = lax.axis_index("az"), lax.axis_index("acq")
     cores = lax.axis_size("acq")
     whole.wait()
+    cut(places, chip, core, cores, stack_ref, chunks)
+
+
+def cut(places, chip, core, cores, stack_ref, chunks):
+    halves, acq_share, _, tiles = stack_ref.shape[:4]
     for owners, chunk in zip(places, chunks):
         blocks = chunk.shape[0] // len(owners)
-        for at, (d, j) in enumerate(owners):
-            first = ((chip ^ d) * cores + (core ^ j)) * blocks
+        for at, (turn, j) in enumerate(owners):
+            owner = chip if turn is None else pick(turns_of(lax.axis_size("az"))[turn], chip)
+            first = (owner * cores + (core ^ j)) * blocks
             for a in range(blocks):
                 for half in range(halves):
                     for t in range(tiles):
@@ -50,14 +58,27 @@
                             chunk[at * blocks + a, half, t, acq] = stack_ref[
                                 half, acq, first + a, t
                             ]
-    for copy in copies:
+
+
+def prepare_kernel(
+    acq_share, relative, groups_in, counts_in, list_in, steer_in, filter_in,
+    first_ref, half_op_ref, op_t_ref, wiener_ref, select_ref, chosen_ref, clear_ref,
+    fmat_ref, groups, counts, list_ref, steer_ref, filter_ref, sems,
+):
+    fetched = [
+        pltpu.make_async_copy(source, target, sems.at[at])
+        for at, (source, target) in enumerate(
+            [
+                (groups_in, groups), (counts_in, counts), (list_in, list_ref),
+                (steer_in, steer_ref), (filter_in, filter_ref),
+            ]
+        )
+    ]
+    for copy in fetched:
+        copy.start()
+    for copy in fetched:
         copy.wait()
 
-
-def prepare_kernel(
-    acq_share, relative, groups, counts, list_ref, steer_ref, filter_ref,
-    first_ref, half_op_ref, op_t_ref, wiener_ref, select_ref, chosen_ref, clear_ref, fmat_ref,
-):
     group_count, _, acquisitions, elevation = steer_ref.shape
     blocks, columns, per_block = list_ref.shape
     depth = 2 * acquisitions
@@ -84,13 +105,17 @@
     half, acq = at // acquisitions, at % acquisitions
     source = acq // acq_share
     if relative:
-        cores = lax.axis_size("acq")
+        cores, chips = lax.axis_size("acq"), lax.axis_size("az")
         chip, core = lax.axis_index("az"), lax.axis_index("acq")
-        source = ((source // cores) ^ chip) * cores + ((source % cores) ^ core)
+        arrival = jnp.zeros_like(source)
+        for turn, targets in enumerate(turns_of(chips)):
+            sender = pick([targets.index(c) for c in range(chips)], chip)
+            arrival = jnp.where(source // cores == sender, turn + 1, arrival)
+        source = arrival * cores + ((source % cores) ^ core)
     place = ((source * 2 + half) * acq_share + acq % acq_share) * columns
     long = lax.broadcasted_iota(jnp.int32, (columns * depth, depth), 0)
     for r in range(columns):
-        g = jnp.max(groups[:, r : r + 1]) - first_group
+        g = jnp.clip(jnp.max(groups[:, r : r + 1]) - first_group, 0, group_count - 1)
         select = jnp.where(long == place + r, 1.0, 0.0).astype(BF16)
         select_ref[r] = select
         real = steer_ref[g, 0]
@@ -201,15 +226,14 @@
             wiener(*part)
         del todo[:count]
 
-    each = len(shares) // ITERS
     for t in range(ITERS):
         if t == 0:
             misfits = picked
         else:
             misfits = [(target_ref[r] - predicted(r)).astype(BF16) for r in range(columns)]
         for r in range(columns):
+            more(1)
             update(r, misfits[r], half_op_ref if t else first_ref, t == 0)
-            more(each // columns)
 
     def copies(a, r, slab):
         where = pl.ds(slab * LANES, LANES)
@@ -298,45 +322,44 @@
                 jax.ShapeDtypeStruct((tiles, blocks * columns * per_block, LANES), BF16),
                 jax.ShapeDtypeStruct((blocks * columns, 8, pixels), F32),
             ],
-            in_specs=[VMEM] * len(small),
+            in_specs=[HBM] * len(small),
             out_specs=[VMEM] * 7,
-            scratch_shapes=[pltpu.VMEM((depth, depth), F32)],
+            scratch_shapes=[pltpu.VMEM((depth, depth), F32)]
+            + [pltpu.VMEM(x.shape, x.dtype) for x in small]
+            + [pltpu.SemaphoreType.DMA((len(small),))],
             cost_estimate=pl.CostEstimate(
                 flops=1_000_000_000, bytes_accessed=4_000_000, transcendentals=0
             ),
             compiler_params=pltpu.CompilerParams(vmem_limit_bytes=16 << 20),
             name="prepare",
-        )(*small)
+        )(*[pltpu.with_memory_space_constraint(x, pltpu.HBM) for x in small])
 
     if pairwise:
         view = image_stack.reshape(halves, acq_share, azb_all, columns, tiles, LANES)
         view = view.transpose(0, 1, 2, 4, 3, 5)
-        turns = sorted(range(1, chips), key=lambda d: (d < chips // 2, d))
-        places = [[(0, 0)], [(0, 1)]] + [[(d, 0), (d, 1)] for d in turns]
+        turns = turns_of(chips)
+        places = [[(None, 0)], [(None, 1)]]
+        places += [[(turn, 0), (turn, 1)] for turn in range(len(turns))]
         unit = (halves, tiles, acq_share, columns, LANES)
         outputs = [
             jax.ShapeDtypeStruct((len(owners) * blocks,) + unit, BF16) for owners in places
         ]
         relayed = pl.pallas_call(
-            lambda *refs: relay_kernel(places, len(small), *refs),
-            out_shape=outputs + [jax.ShapeDtypeStruct(x.shape, x.dtype) for x in small],
-            in_specs=[HBM] * (1 + len(small)),
-            out_specs=[VMEM] * (len(places) + len(small)),
-            scratch_shapes=[
-                pltpu.VMEM(view.shape, BF16),
-                pltpu.SemaphoreType.DMA,
-                pltpu.SemaphoreType.DMA((len(small),)),
-            ],
+            lambda *refs: relay_kernel(places, *refs),
+            out_shape=outputs,
+            in_specs=[HBM],
+            out_specs=[VMEM] * len(places),
+            scratch_shapes=[pltpu.VMEM(view.shape, BF16), pltpu.SemaphoreType.DMA],
             compiler_params=pltpu.CompilerParams(vmem_limit_bytes=4 << 20),
             name="relay",
-        )(*[pltpu.with_memory_space_constraint(x, pltpu.HBM) for x in [view] + small])
-        prepared = prepare(relayed[len(places) :])
+        )(pltpu.with_memory_space_constraint(view, pltpu.HBM))
+        prepared = prepare(small)
         flat = (halves, tiles, acq_share * columns, LANES)
-        chunks = [chunk.reshape((-1,) + flat) for chunk in relayed[: len(places)]]
+        chunks = [chunk.reshape((-1,) + flat) for chunk in relayed]
         got, waiting = {(0, 0): chunks[0]}, {(0, 1): chunks[1]}
-        for d, chunk in zip(turns, chunks[2:]):
-            arrived = lax.ppermute(chunk, "az", [(c, c ^ d) for c in range(chips)])
-            got[d, 0] = waiting[d, 1] = arrived
+        for at, (targets, chunk) in enumerate(zip(turns, chunks[2:])):
+            arrived = lax.ppermute(chunk, "az", list(enumerate(targets)))
+            got[at + 1, 0] = waiting[at + 1, 1] = arrived
         names = list(waiting)
         skips = [waiting[n].shape[0] - blocks for n in names]
         passing = pl.pallas_call(

time: 17.8 us -> 17.2 us (0.966)
  waiting for transfers between devices: 4.92 us -> 2.25 us
  starting transfers between devices: 5.78 us -> 7.23 us
  Pallas kernels: 6.92 us -> 7.57 us
    ppermute x3, waiting for transfers between devices: 3.58 us -> 0.92 us  [shards(): arrived = lax.ppermute(chunk, 'az', list(enumerate(targets)))]
    ppermute x3, starting transfers between devices: 5.71 us -> 7.16 us  [shards(): arrived = lax.ppermute(chunk, 'az', list(enumerate(targets)))]
    pallas_call x1, Pallas kernels: 1.14 us -> 2.2 us  [prepare(): pl.pallas_call(lambda *refs: prepare_kernel(acq_share, pairwise, *refs),...]
    pallas_call x1, Pallas kernels: 4.45 us -> 4.22 us  [shards(): pl.pallas_call(body, out_shape=jax.ShapeDtypeStruct((blocks, columns, ele...]
  transfers between devices with their start and end apart: 4 -> 4, of which waited for: 4 -> 3; matrix products, arithmetic and copies ran while one was open for 0% -> 0% of each run, Pallas kernels for 7% -> 13%
where the time goes in v3:
time: 17.2 us; the launch traced here: 17.1 us
  Pallas kernels  7.57 us (44%)
  starting transfers between devices  7.23 us (42%)
  waiting for transfers between devices  2.25 us (13%)
    ppermute x3, starting transfers between devices, shards(): arrived = lax.ppermute(chunk, 'az', list(enumerate(targets)))  7.16 us
    pallas_call x1, Pallas kernels, shards(): pl.pallas_call(body, out_shape=jax.ShapeDtypeStruct((blocks, columns, ele...  4.22 us
    pallas_call x1, Pallas kernels, prepare(): pl.pallas_call(lambda *refs: prepare_kernel(acq_share, pairwise, *refs),...  2.2 us
    ppermute x1, waiting for transfers between devices, shards(): passed = lax.ppermute(passing, 'acq', [(0, 1), (1, 0)])  1.33 us
    pallas_call x1, Pallas kernels, shards(): pl.pallas_call(lambda *refs: relay_kernel(places, *refs), out_shape=outpu...  1.14 us
    ppermute x3, waiting for transfers between devices, shards(): arrived = lax.ppermute(chunk, 'az', list(enumerate(targets)))  0.92 us
  transfers between devices with their start and end apart: 4, of which 3 were waited for; matrix products, arithmetic and copies ran while one was open for 0% of the time, Pallas kernels for 13%

profile of v3, /device:TPU:0, one launch (start us, length us, event | category | flops | bytes accessed | tf_op | source)
XLA Modules:
  0.0 17.1 jit_solution(4002194420328335019)
XLA Ops:
  0.0 1.1 %relay.1 = (bf16[2,2,2,8,2,128]{5,4,3,2,1,0:T(2,128)(2,1)S(1)}, bf16[2,2,2,8,2,128]{5,4,3,2,1,0:T(2,128)(2,1)S(1)}, bf16[4,2,2,8,2,128]{5,4,3,2,1,0:T(2,128)(2,1...) custom-call(bf16[2,8,16,2,2,128]{5,4,3,2,1,0:T(2,128)(2,1)} %bitcast.16), custom_call_target="tpu_custom_call" | custom-call | tf_op jit(solution)/shard_map/relay/pallas_call | solution.py:347
  1.2 3.1 %collective-permute-start = (bf16[4,2,2,16,128]{4,3,2,1,0:T(8,128)(2,1)S(1)}, bf16[4,2,2,16,128]{4,3,2,1,0:T(8,128)(2,1)S(1)}, u32[]{:S(2)}, u32[]{:S(2)}) collective-permute-start(bf16[4,2,2,16,128]{4,3,2,1,0:T(8,128)(2,1)S(1)} %bitcast.14), channel_id=1, source_target_pairs={{0,4},{4,12},{8,0},{12,8},{1,5},{5,13},{9,1},{13,9},{2,6},{6,14},{... | collective-permute-start | bytes 196616 | tf_op jit(solution)/shard_map/ppermute | solution.py:361
  4.3 2.5 %collective-permute-start.1 = (bf16[4,2,2,16,128]{4,3,2,1,0:T(8,128)(2,1)S(1)}, bf16[4,2,2,16,128]{4,3,2,1,0:T(8,128)(2,1)S(1)}, u32[]{:S(2)}, u32[]{:S(2)}) collective-permute-start(bf16[4,2,2,16,128]{4,3,2,1,0:T(8,128)(2,1)S(1)} %bitcast.13), channel_id=1, source_target_pairs={{0,12},{4,8},{8,4},{12,0},{1,13},{5,9},{9,5},{13,1},{2,14},{6,10},... | collective-permute-start | bytes 196616 | tf_op jit(solution)/shard_map/ppermute | solution.py:361
  6.7 1.6 %collective-permute-start.2 = (bf16[4,2,2,16,128]{4,3,2,1,0:T(8,128)(2,1)S(1)}, bf16[4,2,2,16,128]{4,3,2,1,0:T(8,128)(2,1)S(1)}, u32[]{:S(2)}, u32[]{:S(2)}) collective-permute-start(bf16[4,2,2,16,128]{4,3,2,1,0:T(8,128)(2,1)S(1)} %bitcast.12), channel_id=1, source_target_pairs={{0,8},{4,0},{8,12},{12,4},{1,9},{5,1},{9,13},{13,5},{2,10},{6,2},{... | collective-permute-start | bytes 196616 | tf_op jit(solution)/shard_map/ppermute | solution.py:361
  8.3 2.2 %prepare.1 = (bf16[2,8,256,128]{3,2,1,0:T(8,128)(2,1)S(1)}, bf16[2,8,128,128]{3,2,1,0:T(8,128)(2,1)S(1)}, bf16[2,4,256,128]{3,2,1,0:T(8,128)(2,1)S(1)}, bf16[2,2...) custom-call(s32[1,2]{1,0:T(1,128)} %bitcast.17, ...), custom_call_target="tpu_custom_call" | custom-call | flops 1000000000 | bytes 4000000 | tf_op jit(solution)/shard_map/prepare/pallas_call | solution.py:312
  10.5 0.0 collective-permute-done.refs_1_
  10.5 0.7 %collective-permute-done.1.refs_2_ = bf16[4,2,2,16,128]{4,3,2,1,0:T(8,128)(2,1)S(1)} collective-permute-done((bf16[4,2,2,16,128]{4,3,2,1,0:T(8,128)(2,1)S(1)}, bf16[4,2,2,16,128]{4,3,2,1,0:T(8,128)(2,1)S(1)}, u32[]{:S(2)}, u32[]{:S(2)}) %collective-permute-start.1) | collective-permute-done | bytes 65568 | tf_op jit(solution)/shard_map/ppermute | solution.py:361
  11.2 0.2 %collective-permute-done.2.refs_3_ = bf16[4,2,2,16,128]{4,3,2,1,0:T(8,128)(2,1)S(1)} collective-permute-done((bf16[4,2,2,16,128]{4,3,2,1,0:T(8,128)(2,1)S(1)}, bf16[4,2,2,16,128]{4,3,2,1,0:T(8,128)(2,1)S(1)}, u32[]{:S(2)}, u32[]{:S(2)}) %collective-permute-start.2) | collective-permute-done | bytes 65568 | tf_op jit(solution)/shard_map/ppermute | solution.py:361
  11.5 0.1 collective-permute-start.3
  11.5 1.3 %collective-permute-done.3 = bf16[8,2,2,16,128]{4,3,2,1,0:T(8,128)(2,1)S(1)} collective-permute-done((bf16[8,2,2,16,128]{4,3,2,1,0:T(8,128)(2,1)S(1)}, bf16[8,2,2,16,128]{4,3,2,1,0:T(8,128)(2,1)S(1)}, u32[]{:S(2)}, u32[]{:S(2)}) %collective-permute-start.3) | collective-permute-done | bytes 131104 | tf_op jit(solution)/shard_map/ppermute | solution.py:374
  12.9 4.2 %profiles.1 = bf16[2,2,512,256]{3,2,1,0:T(8,128)(2,1)} custom-call(bf16[2,2,2,16,128]{4,3,2,1,0:T(8,128)(2,1)S(1)} %bitcast.15, bf16[4,2,2,16,128]{4,3,2,1,0:T(8,128)(2,1)S(1)} %collective-permute-done.refs_1_, bf16[4,2,2,16,128]{4,3,2,1,0:T(8,128)(2,1)S(1)} %collective-permute-done.1.refs_2_, ...), custom_call_target="tpu_custom_call" | custom-call | flops 2000000000 | bytes 4000000 | tf_op jit(solution)/shard_map/profiles/pallas_call | solution.py:394
  (1 shorter events, 0.0 us)
Async XLA Ops:
  1.2 9.4 %collective-permute-start = (bf16[4,2,2,16,128]{4,3,2,1,0:T(8,128)(2,1)S(1)}, bf16[4,2,2,16,128]{4,3,2,1,0:T(8,128)(2,1)S(1)}, u32[]{:S(2)}, u32[]{:S(2)}) collective-permute-start(bf16[4,2,2,16,128]{4,3,2,1,0:T(8,128)(2,1)S(1)} %bitcast.14), channel_id=1, source_target_pairs={{0,4},{4,12},{8,0},{12,8},{1,5},{5,13},{9,1},{13,9},{2,6},{6,14},{... | collective-permute-start | bytes 196616 | tf_op jit(solution)/shard_map/ppermute | solution.py:361
  4.3 7.0 %collective-permute-start.1 = (bf16[4,2,2,16,128]{4,3,2,1,0:T(8,128)(2,1)S(1)}, bf16[4,2,2,16,128]{4,3,2,1,0:T(8,128)(2,1)S(1)}, u32[]{:S(2)}, u32[]{:S(2)}) collective-permute-start(bf16[4,2,2,16,128]{4,3,2,1,0:T(8,128)(2,1)S(1)} %bitcast.13), channel_id=1, source_target_pairs={{0,12},{4,8},{8,4},{12,0},{1,13},{5,9},{9,5},{13,1},{2,14},{6,10},... | collective-permute-start | bytes 196616 | tf_op jit(solution)/shard_map/ppermute | solution.py:361
  6.7 4.7 %collective-permute-start.2 = (bf16[4,2,2,16,128]{4,3,2,1,0:T(8,128)(2,1)S(1)}, bf16[4,2,2,16,128]{4,3,2,1,0:T(8,128)(2,1)S(1)}, u32[]{:S(2)}, u32[]{:S(2)}) collective-permute-start(bf16[4,2,2,16,128]{4,3,2,1,0:T(8,128)(2,1)S(1)} %bitcast.12), channel_id=1, source_target_pairs={{0,8},{4,0},{8,12},{12,4},{1,9},{5,1},{9,13},{13,5},{2,10},{6,2},{... | collective-permute-start | bytes 196616 | tf_op jit(solution)/shard_map/ppermute | solution.py:361
  11.5 1.4 %collective-permute-start.3 = (bf16[8,2,2,16,128]{4,3,2,1,0:T(8,128)(2,1)S(1)}, bf16[8,2,2,16,128]{4,3,2,1,0:T(8,128)(2,1)S(1)}, u32[]{:S(2)}, u32[]{:S(2)}) collective-permute-start(bf16[8,2,2,16,128]{4,3,2,1,0:T(8,128)(2,1)S(1)} %join.1), channel_id=1, source_target_pairs={{0,1},{1,0},{2,3},{3,2},{4,5},{5,4},{6,7},{7,6},{8,9},{9,8},{10,11... | collective-permute-start | bytes 393224 | tf_op jit(solution)/shard_map/ppermute | solution.py:374

commit v4 on v3

--- a/solution.py
+++ b/solution.py
@@ -34,14 +34,23 @@
     return sum(jnp.where(index == at, value, 0) for at, value in enumerate(table))
 
 
-def relay_kernel(places, x_ref, *refs):
-    chunks, stack_ref, sem = refs[:-2], refs[-2], refs[-1]
+def relay_kernel(places, extra, x_ref, *refs):
+    small, refs = refs[:extra], refs[extra:]
+    chunks, fetched, (stack_ref, sem, sems) = refs[: len(places)], refs[len(places) : -3], refs[-3:]
     whole = pltpu.make_async_copy(x_ref, stack_ref, sem)
     whole.start()
+    copies = [
+        pltpu.make_async_copy(source, target, sems.at[at])
+        for at, (source, target) in enumerate(zip(small, fetched))
+    ]
+    for copy in copies:
+        copy.start()
     chip, core = lax.axis_index("az"), lax.axis_index("acq")
     cores = lax.axis_size("acq")
     whole.wait()
     cut(places, chip, core, cores, stack_ref, chunks)
+    for copy in copies:
+        copy.wait()
 
 
 def cut(places, chip, core, cores, stack_ref, chunks):
@@ -61,24 +70,9 @@
 
 
 def prepare_kernel(
-    acq_share, relative, groups_in, counts_in, list_in, steer_in, filter_in,
-    first_ref, half_op_ref, op_t_ref, wiener_ref, select_ref, chosen_ref, clear_ref,
-    fmat_ref, groups, counts, list_ref, steer_ref, filter_ref, sems,
+    acq_share, relative, groups, counts, list_ref, steer_ref, filter_ref,
+    first_ref, half_op_ref, op_t_ref, wiener_ref, select_ref, chosen_ref, clear_ref, fmat_ref,
 ):
-    fetched = [
-        pltpu.make_async_copy(source, target, sems.at[at])
-        for at, (source, target) in enumerate(
-            [
-                (groups_in, groups), (counts_in, counts), (list_in, list_ref),
-                (steer_in, steer_ref), (filter_in, filter_ref),
-            ]
-        )
-    ]
-    for copy in fetched:
-        copy.start()
-    for copy in fetched:
-        copy.wait()
-
     group_count, _, acquisitions, elevation = steer_ref.shape
     blocks, columns, per_block = list_ref.shape
     depth = 2 * acquisitions
@@ -322,17 +316,15 @@
                 jax.ShapeDtypeStruct((tiles, blocks * columns * per_block, LANES), BF16),
                 jax.ShapeDtypeStruct((blocks * columns, 8, pixels), F32),
             ],
-            in_specs=[HBM] * len(small),
+            in_specs=[VMEM] * len(small),
             out_specs=[VMEM] * 7,
-            scratch_shapes=[pltpu.VMEM((depth, depth), F32)]
-            + [pltpu.VMEM(x.shape, x.dtype) for x in small]
-            + [pltpu.SemaphoreType.DMA((len(small),))],
+            scratch_shapes=[pltpu.VMEM((depth, depth), F32)],
             cost_estimate=pl.CostEstimate(
                 flops=1_000_000_000, bytes_accessed=4_000_000, transcendentals=0
             ),
             compiler_params=pltpu.CompilerParams(vmem_limit_bytes=16 << 20),
             name="prepare",
-        )(*[pltpu.with_memory_space_constraint(x, pltpu.HBM) for x in small])
+        )(*small)
 
     if pairwise:
         view = image_stack.reshape(halves, acq_share, azb_all, columns, tiles, LANES)
@@ -344,41 +336,52 @@
         outputs = [
             jax.ShapeDtypeStruct((len(owners) * blocks,) + unit, BF16) for owners in places
         ]
+        tiny = [x for x in small if x is not steering]
         relayed = pl.pallas_call(
-            lambda *refs: relay_kernel(places, *refs),
-            out_shape=outputs,
-            in_specs=[HBM],
-            out_specs=[VMEM] * len(places),
-            scratch_shapes=[pltpu.VMEM(view.shape, BF16), pltpu.SemaphoreType.DMA],
+            lambda *refs: relay_kernel(places, len(tiny), *refs),
+            out_shape=outputs + [jax.ShapeDtypeStruct(x.shape, x.dtype) for x in tiny],
+            in_specs=[HBM] * (1 + len(tiny)),
+            out_specs=[VMEM] * (len(places) + len(tiny)),
+            scratch_shapes=[
+                pltpu.VMEM(view.shape, BF16),
+                pltpu.SemaphoreType.DMA,
+                pltpu.SemaphoreType.DMA((len(tiny),)),
+            ],
             compiler_params=pltpu.CompilerParams(vmem_limit_bytes=4 << 20),
             name="relay",
-        )(pltpu.with_memory_space_constraint(view, pltpu.HBM))
-        prepared = prepare(small)
+        )(*[pltpu.with_memory_space_constraint(x, pltpu.HBM) for x in [view] + tiny])
+        groups, counts, listed, filters = relayed[len(places) :]
+        prepared = prepare([groups, counts, listed, steering, filters])
         flat = (halves, tiles, acq_share * columns, LANES)
-        chunks = [chunk.reshape((-1,) + flat) for chunk in relayed]
+        chunks = [chunk.reshape((-1,) + flat) for chunk in relayed[: len(places)]]
         got, waiting = {(0, 0): chunks[0]}, {(0, 1): chunks[1]}
         for at, (targets, chunk) in enumerate(zip(turns, chunks[2:])):
             arrived = lax.ppermute(chunk, "az", list(enumerate(targets)))
             got[at + 1, 0] = waiting[at + 1, 1] = arrived
         names = list(waiting)
-        skips = [waiting[n].shape[0] - blocks for n in names]
-        passing = pl.pallas_call(
-            lambda *refs: join_kernel(skips, *refs),
-            out_shape=jax.ShapeDtypeStruct((len(names) * blocks,) + flat, BF16),
-            in_specs=[VMEM] * len(names),
-            out_specs=VMEM,
-            compiler_params=pltpu.CompilerParams(vmem_limit_bytes=2 << 20),
-            name="join",
-        )(*[waiting[n] for n in names])
-        passing, prepared = lax.optimization_barrier((passing, prepared))
-        passed = lax.ppermute(passing, "acq", [(0, 1), (1, 0)])
+        passed = []
+        for group in (names[:2], names[2:]):
+            skips = [waiting[n].shape[0] - blocks for n in group]
+            passing = pl.pallas_call(
+                lambda *refs: join_kernel(skips, *refs),
+                out_shape=jax.ShapeDtypeStruct((len(group) * blocks,) + flat, BF16),
+                in_specs=[VMEM] * len(group),
+                out_specs=VMEM,
+                compiler_params=pltpu.CompilerParams(vmem_limit_bytes=2 << 20),
+                name="join",
+            )(*[waiting[n] for n in group])
+            if not passed:
+                passing, prepared = lax.optimization_barrier((passing, prepared))
+            array = lax.ppermute(passing, "acq", [(0, 1), (1, 0)])
+            passed.append((group, array))
         arrays, order = [], {}
         for place, array in got.items():
             order[place] = (len(arrays), ())
             arrays.append(array)
-        for at, place in enumerate(names):
-            order[place] = (len(arrays), (at,))
-        arrays.append(passed.reshape((len(names), blocks) + flat))
+        for group, array in passed:
+            for at, place in enumerate(group):
+                order[place] = (len(arrays), (at,))
+            arrays.append(array.reshape((len(group), blocks) + flat))
         order = [order[d, j] for d in range(chips) for j in range(cores)]
         lead = arrays
         body = lambda *refs: pieces_kernel(len(arrays), order, *refs)

time: 17.2 us -> 17.4 us (1.012)
  Pallas kernels: 7.57 us -> 6.66 us
  waiting for transfers between devices: 2.25 us -> 2.87 us
  starting transfers between devices: 7.23 us -> 7.71 us
    ppermute x3, waiting for transfers between devices: 0.92 us -> 1.97 us  [shards(): arrived = lax.ppermute(chunk, 'az', list(enumerate(targets)))]
    pallas_call x1, Pallas kernels: 2.2 us -> 1.15 us  [prepare(): pl.pallas_call(lambda *refs: prepare_kernel(acq_share, pairwise, *refs),...]
    ppermute x1 -> x2, starting transfers between devices: 0.07 us -> 0.56 us  [shards(): array = lax.ppermute(passing, 'acq', [(0, 1), (1, 0)])]
    ppermute x1 -> x2, waiting for transfers between devices: 1.33 us -> 0.9 us  [shards(): array = lax.ppermute(passing, 'acq', [(0, 1), (1, 0)])]
  transfers between devices with their start and end apart: 4 -> 5, of which waited for: 3 -> 4; matrix products, arithmetic and copies ran while one was open for 0% -> 0% of each run, Pallas kernels for 13% -> 7%
where the time goes in v4:
time: 17.4 us; the launch traced here: 17.3 us
  starting transfers between devices  7.71 us (44%)
  Pallas kernels  6.66 us (38%)
  waiting for transfers between devices  2.87 us (16%)
    ppermute x3, starting transfers between devices, shards(): arrived = lax.ppermute(chunk, 'az', list(enumerate(targets)))  7.16 us
    pallas_call x1, Pallas kernels, shards(): pl.pallas_call(body, out_shape=jax.ShapeDtypeStruct((blocks, columns, ele...  4.22 us
    ppermute x3, waiting for transfers between devices, shards(): arrived = lax.ppermute(chunk, 'az', list(enumerate(targets)))  1.97 us
    pallas_call x1, Pallas kernels, shards(): pl.pallas_call(lambda *refs: relay_kernel(places, len(tiny), *refs), out_...  1.28 us
    pallas_call x1, Pallas kernels, prepare(): pl.pallas_call(lambda *refs: prepare_kernel(acq_share, pairwise, *refs),...  1.15 us
    ppermute x2, waiting for transfers between devices, shards(): array = lax.ppermute(passing, 'acq', [(0, 1), (1, 0)])  0.9 us
    ppermute x2, starting transfers between devices, shards(): array = lax.ppermute(passing, 'acq', [(0, 1), (1, 0)])  0.56 us
  transfers between devices with their start and end apart: 5, of which 4 were waited for; matrix products, arithmetic and copies ran while one was open for 0% of the time, Pallas kernels for 7%

profile of v4, /device:TPU:0, one launch (start us, length us, event | category | flops | bytes accessed | tf_op | source)
XLA Modules:
  0.0 17.3 jit_solution(9477085455603379747)
XLA Ops:
  0.0 0.0 copy-start
  0.0 1.3 %relay.1 = (bf16[2,2,2,8,2,128]{5,4,3,2,1,0:T(2,128)(2,1)S(1)}, bf16[2,2,2,8,2,128]{5,4,3,2,1,0:T(2,128)(2,1)S(1)}, bf16[4,2,2,8,2,128]{5,4,3,2,1,0:T(2,128)(2,1...) custom-call(bf16[2,8,16,2,2,128]{5,4,3,2,1,0:T(2,128)(2,1)} %bitcast, ...), custom_call_target="tpu_custom_call" | custom-call | tf_op jit(solution)/shard_map/relay/pallas_call | solution.py:340
  1.3 3.1 %collective-permute-start = (bf16[4,2,2,16,128]{4,3,2,1,0:T(8,128)(2,1)S(1)}, bf16[4,2,2,16,128]{4,3,2,1,0:T(8,128)(2,1)S(1)}, u32[]{:S(2)}, u32[]{:S(2)}) collective-permute-start(bf16[4,2,2,16,128]{4,3,2,1,0:T(8,128)(2,1)S(1)} %bitcast.12), channel_id=1, source_target_pairs={{0,4},{4,12},{8,0},{12,8},{1,5},{5,13},{9,1},{13,9},{2,6},{6,14},{... | collective-permute-start | bytes 196616 | tf_op jit(solution)/shard_map/ppermute | solution.py:359
  4.4 2.5 %collective-permute-start.1 = (bf16[4,2,2,16,128]{4,3,2,1,0:T(8,128)(2,1)S(1)}, bf16[4,2,2,16,128]{4,3,2,1,0:T(8,128)(2,1)S(1)}, u32[]{:S(2)}, u32[]{:S(2)}) collective-permute-start(bf16[4,2,2,16,128]{4,3,2,1,0:T(8,128)(2,1)S(1)} %bitcast.15), channel_id=1, source_target_pairs={{0,12},{4,8},{8,4},{12,0},{1,13},{5,9},{9,5},{13,1},{2,14},{6,10},... | collective-permute-start | bytes 196616 | tf_op jit(solution)/shard_map/ppermute | solution.py:359
  6.9 1.6 %collective-permute-start.2 = (bf16[4,2,2,16,128]{4,3,2,1,0:T(8,128)(2,1)S(1)}, bf16[4,2,2,16,128]{4,3,2,1,0:T(8,128)(2,1)S(1)}, u32[]{:S(2)}, u32[]{:S(2)}) collective-permute-start(bf16[4,2,2,16,128]{4,3,2,1,0:T(8,128)(2,1)S(1)} %bitcast.13), channel_id=1, source_target_pairs={{0,8},{4,0},{8,12},{12,4},{1,9},{5,1},{9,13},{13,5},{2,10},{6,2},{... | collective-permute-start | bytes 196616 | tf_op jit(solution)/shard_map/ppermute | solution.py:359
  8.4 0.0 copy-done
  8.4 1.1 %prepare.1 = (bf16[2,8,256,128]{3,2,1,0:T(8,128)(2,1)S(1)}, bf16[2,8,128,128]{3,2,1,0:T(8,128)(2,1)S(1)}, bf16[2,4,256,128]{3,2,1,0:T(8,128)(2,1)S(1)}, bf16[2,2...) custom-call(s32[1,2]{1,0:T(1,128)S(1)} %get-tuple-element.34.refs_0_, ...), custom_call_target="tpu_custom_call" | custom-call | flops 1000000000 | bytes 4000000 | tf_op jit(solution)/shard_map/prepare/pallas_call | solution.py:306
  9.6 1.7 %collective-permute-done.1.refs_0_.refs_2_ = bf16[4,2,2,16,128]{4,3,2,1,0:T(8,128)(2,1)S(1)} collective-permute-done((bf16[4,2,2,16,128]{4,3,2,1,0:T(8,128)(2,1)S(1)}, bf16[4,2,2,16,128]{4,3,2,1,0:T(8,128)(2,1)S(1)}, u32[]{:S(2)}, u32[]{:S(2)}) %collective-permute-start.1) | collective-permute-done | bytes 65568 | tf_op jit(solution)/shard_map/ppermute | solution.py:359
  11.3 0.2 %collective-permute-done.2.refs_1_.refs_3_ = bf16[4,2,2,16,128]{4,3,2,1,0:T(8,128)(2,1)S(1)} collective-permute-done((bf16[4,2,2,16,128]{4,3,2,1,0:T(8,128)(2,1)S(1)}, bf16[4,2,2,16,128]{4,3,2,1,0:T(8,128)(2,1)S(1)}, u32[]{:S(2)}, u32[]{:S(2)}) %collective-permute-start.2) | collective-permute-done | bytes 65568 | tf_op jit(solution)/shard_map/ppermute | solution.py:359
  11.6 0.0 collective-permute-start.4
  11.6 0.0 collective-permute-done.refs_1_
  11.6 0.6 %collective-permute-start.3 = (bf16[4,2,2,16,128]{4,3,2,1,0:T(8,128)(2,1)S(1)}, bf16[4,2,2,16,128]{4,3,2,1,0:T(8,128)(2,1)S(1)}, u32[]{:S(2)}, u32[]{:S(2)}) collective-permute-start(bf16[4,2,2,16,128]{4,3,2,1,0:T(8,128)(2,1)S(1)} %join.2), channel_id=1, source_target_pairs={{0,1},{1,0},{2,3},{3,2},{4,5},{5,4},{6,7},{7,6},{8,9},{9,8},{10,11... | collective-permute-start | bytes 196616 | tf_op jit(solution)/shard_map/ppermute | solution.py:375
  12.2 0.7 %collective-permute-done.4 = bf16[4,2,2,16,128]{4,3,2,1,0:T(8,128)(2,1)S(1)} collective-permute-done((bf16[4,2,2,16,128]{4,3,2,1,0:T(8,128)(2,1)S(1)}, bf16[4,2,2,16,128]{4,3,2,1,0:T(8,128)(2,1)S(1)}, u32[]{:S(2)}, u32[]{:S(2)}) %collective-permute-start.4) | collective-permute-done | bytes 65568 | tf_op jit(solution)/shard_map/ppermute | solution.py:375
  12.8 0.2 %collective-permute-done.3 = bf16[4,2,2,16,128]{4,3,2,1,0:T(8,128)(2,1)S(1)} collective-permute-done((bf16[4,2,2,16,128]{4,3,2,1,0:T(8,128)(2,1)S(1)}, bf16[4,2,2,16,128]{4,3,2,1,0:T(8,128)(2,1)S(1)}, u32[]{:S(2)}, u32[]{:S(2)}) %collective-permute-start.3) | collective-permute-done | bytes 65568 | tf_op jit(solution)/shard_map/ppermute | solution.py:375
  13.1 4.2 %profiles.1 = bf16[2,2,512,256]{3,2,1,0:T(8,128)(2,1)} custom-call(bf16[2,2,2,16,128]{4,3,2,1,0:T(8,128)(2,1)S(1)} %bitcast.17, bf16[4,2,2,16,128]{4,3,2,1,0:T(8,128)(2,1)S(1)} %collective-permute-done.refs_1_, bf16[4,2,2,16,128]{4,3,2,1,0:T(8,128)(2,1)S(1)} %collective-permute-done.1.refs_0_.refs_2_, ...), custom_call_target="tpu_custom_call" | custom-call | flops 2000000000 | bytes 4000000 | tf_op jit(solution)/shard_map/profiles/pallas_call | solution.py:397
  (2 shorter events, 0.0 us)
Async XLA Ops:
  0.0 8.4 %copy-start = (bf16[2,2,64,512]{3,2,1,0:T(8,128)(2,1)S(1)}, bf16[2,2,64,512]{3,2,1,0:T(8,128)(2,1)}, u32[]{:S(2)}) copy-start(bf16[2,2,64,512]{3,2,1,0:T(8,128)(2,1)} %refs_3_.3) | copy-start | bytes 786436
  1.3 10.3 %collective-permute-start = (bf16[4,2,2,16,128]{4,3,2,1,0:T(8,128)(2,1)S(1)}, bf16[4,2,2,16,128]{4,3,2,1,0:T(8,128)(2,1)S(1)}, u32[]{:S(2)}, u32[]{:S(2)}) collective-permute-start(bf16[4,2,2,16,128]{4,3,2,1,0:T(8,128)(2,1)S(1)} %bitcast.12), channel_id=1, source_target_pairs={{0,4},{4,12},{8,0},{12,8},{1,5},{5,13},{9,1},{13,9},{2,6},{6,14},{... | collective-permute-start | bytes 196616 | tf_op jit(solution)/shard_map/ppermute | solution.py:359
  4.4 7.0 %collective-permute-start.1 = (bf16[4,2,2,16,128]{4,3,2,1,0:T(8,128)(2,1)S(1)}, bf16[4,2,2,16,128]{4,3,2,1,0:T(8,128)(2,1)S(1)}, u32[]{:S(2)}, u32[]{:S(2)}) collective-permute-start(bf16[4,2,2,16,128]{4,3,2,1,0:T(8,128)(2,1)S(1)} %bitcast.15), channel_id=1, source_target_pairs={{0,12},{4,8},{8,4},{12,0},{1,13},{5,9},{9,5},{13,1},{2,14},{6,10},... | collective-permute-start | bytes 196616 | tf_op jit(solution)/shard_map/ppermute | solution.py:359
  6.9 4.7 %collective-permute-start.2 = (bf16[4,2,2,16,128]{4,3,2,1,0:T(8,128)(2,1)S(1)}, bf16[4,2,2,16,128]{4,3,2,1,0:T(8,128)(2,1)S(1)}, u32[]{:S(2)}, u32[]{:S(2)}) collective-permute-start(bf16[4,2,2,16,128]{4,3,2,1,0:T(8,128)(2,1)S(1)} %bitcast.13), channel_id=1, source_target_pairs={{0,8},{4,0},{8,12},{12,4},{1,9},{5,1},{9,13},{13,5},{2,10},{6,2},{... | collective-permute-start | bytes 196616 | tf_op jit(solution)/shard_map/ppermute | solution.py:359
  11.6 1.3 %collective-permute-start.4 = (bf16[4,2,2,16,128]{4,3,2,1,0:T(8,128)(2,1)S(1)}, bf16[4,2,2,16,128]{4,3,2,1,0:T(8,128)(2,1)S(1)}, u32[]{:S(2)}, u32[]{:S(2)}) collective-permute-start(bf16[4,2,2,16,128]{4,3,2,1,0:T(8,128)(2,1)S(1)} %join.3), channel_id=1, source_target_pairs={{0,1},{1,0},{2,3},{3,2},{4,5},{5,4},{6,7},{7,6},{8,9},{9,8},{10,11... | collective-permute-start | bytes 196616 | tf_op jit(solution)/shard_map/ppermute | solution.py:375
  11.6 1.5 %collective-permute-start.3 = (bf16[4,2,2,16,128]{4,3,2,1,0:T(8,128)(2,1)S(1)}, bf16[4,2,2,16,128]{4,3,2,1,0:T(8,128)(2,1)S(1)}, u32[]{:S(2)}, u32[]{:S(2)}) collective-permute-start(bf16[4,2,2,16,128]{4,3,2,1,0:T(8,128)(2,1)S(1)} %join.2), channel_id=1, source_target_pairs={{0,1},{1,0},{2,3},{3,2},{4,5},{5,4},{6,7},{7,6},{8,9},{9,8},{10,11... | collective-permute-start | bytes 196616 | tf_op jit(solution)/shard_map/ppermute | solution.py:375

commit v5 on v3

--- a/solution.py
+++ b/solution.py
@@ -361,24 +361,29 @@
             arrived = lax.ppermute(chunk, "az", list(enumerate(targets)))
             got[at + 1, 0] = waiting[at + 1, 1] = arrived
         names = list(waiting)
-        skips = [waiting[n].shape[0] - blocks for n in names]
-        passing = pl.pallas_call(
-            lambda *refs: join_kernel(skips, *refs),
-            out_shape=jax.ShapeDtypeStruct((len(names) * blocks,) + flat, BF16),
-            in_specs=[VMEM] * len(names),
-            out_specs=VMEM,
-            compiler_params=pltpu.CompilerParams(vmem_limit_bytes=2 << 20),
-            name="join",
-        )(*[waiting[n] for n in names])
-        passing, prepared = lax.optimization_barrier((passing, prepared))
-        passed = lax.ppermute(passing, "acq", [(0, 1), (1, 0)])
+        passed = []
+        for group in (names[:2], names[2:]):
+            skips = [waiting[n].shape[0] - blocks for n in group]
+            passing = pl.pallas_call(
+                lambda *refs: join_kernel(skips, *refs),
+                out_shape=jax.ShapeDtypeStruct((len(group) * blocks,) + flat, BF16),
+                in_specs=[VMEM] * len(group),
+                out_specs=VMEM,
+                compiler_params=pltpu.CompilerParams(vmem_limit_bytes=2 << 20),
+                name="join",
+            )(*[waiting[n] for n in group])
+            if not passed:
+                passing, prepared = lax.optimization_barrier((passing, prepared))
+            array = lax.ppermute(passing, "acq", [(0, 1), (1, 0)])
+            passed.append((group, array))
         arrays, order = [], {}
         for place, array in got.items():
             order[place] = (len(arrays), ())
             arrays.append(array)
-        for at, place in enumerate(names):
-            order[place] = (len(arrays), (at,))
-        arrays.append(passed.reshape((len(names), blocks) + flat))
+        for group, array in passed:
+            for at, place in enumerate(group):
+                order[place] = (len(arrays), (at,))
+            arrays.append(array.reshape((len(group), blocks) + flat))
         order = [order[d, j] for d in range(chips) for j in range(cores)]
         lead = arrays
         body = lambda *refs: pieces_kernel(len(arrays), order, *refs)

time: 17.2 us -> 17.3 us (level)
  starting transfers between devices: 7.23 us -> 7.71 us
  waiting for transfers between devices: 2.25 us -> 1.83 us
    ppermute x1 -> x2, starting transfers between devices: 0.07 us -> 0.56 us  [shards(): array = lax.ppermute(passing, 'acq', [(0, 1), (1, 0)])]
    ppermute x1 -> x2, waiting for transfers between devices: 1.33 us -> 0.9 us  [shards(): array = lax.ppermute(passing, 'acq', [(0, 1), (1, 0)])]
  transfers between devices with their start and end apart: 4 -> 5, of which waited for: 3 -> 4; matrix products, arithmetic and copies ran while one was open for 0% -> 0% of each run, Pallas kernels for 13% -> 13%
where the time goes in v5:
time: 17.3 us; the launch traced here: 17.2 us
  starting transfers between devices  7.71 us (45%)
  Pallas kernels  7.57 us (44%)
  waiting for transfers between devices  1.83 us (11%)
    ppermute x3, starting transfers between devices, shards(): arrived = lax.ppermute(chunk, 'az', list(enumerate(targets)))  7.16 us
    pallas_call x1, Pallas kernels, shards(): pl.pallas_call(body, out_shape=jax.ShapeDtypeStruct((blocks, columns, ele...  4.22 us
    pallas_call x1, Pallas kernels, prepare(): pl.pallas_call(lambda *refs: prepare_kernel(acq_share, pairwise, *refs),...  2.2 us
    pallas_call x1, Pallas kernels, shards(): pl.pallas_call(lambda *refs: relay_kernel(places, *refs), out_shape=outpu...  1.14 us
    ppermute x3, waiting for transfers between devices, shards(): arrived = lax.ppermute(chunk, 'az', list(enumerate(targets)))  0.93 us
    ppermute x2, waiting for transfers between devices, shards(): array = lax.ppermute(passing, 'acq', [(0, 1), (1, 0)])  0.9 us
    ppermute x2, starting transfers between devices, shards(): array = lax.ppermute(passing, 'acq', [(0, 1), (1, 0)])  0.56 us
  transfers between devices with their start and end apart: 5, of which 4 were waited for; matrix products, arithmetic and copies ran while one was open for 0% of the time, Pallas kernels for 13%

profile of v5, /device:TPU:0, one launch (start us, length us, event | category | flops | bytes accessed | tf_op | source)
XLA Modules:
  0.0 17.2 jit_solution(11116311327333088512)
XLA Ops:
  0.0 1.1 %relay.1 = (bf16[2,2,2,8,2,128]{5,4,3,2,1,0:T(2,128)(2,1)S(1)}, bf16[2,2,2,8,2,128]{5,4,3,2,1,0:T(2,128)(2,1)S(1)}, bf16[4,2,2,8,2,128]{5,4,3,2,1,0:T(2,128)(2,1...) custom-call(bf16[2,8,16,2,2,128]{5,4,3,2,1,0:T(2,128)(2,1)} %bitcast.18), custom_call_target="tpu_custom_call" | custom-call | tf_op jit(solution)/shard_map/relay/pallas_call | solution.py:347
  1.2 3.1 %collective-permute-start = (bf16[4,2,2,16,128]{4,3,2,1,0:T(8,128)(2,1)S(1)}, bf16[4,2,2,16,128]{4,3,2,1,0:T(8,128)(2,1)S(1)}, u32[]{:S(2)}, u32[]{:S(2)}) collective-permute-start(bf16[4,2,2,16,128]{4,3,2,1,0:T(8,128)(2,1)S(1)} %bitcast.12), channel_id=1, source_target_pairs={{0,4},{4,12},{8,0},{12,8},{1,5},{5,13},{9,1},{13,9},{2,6},{6,14},{... | collective-permute-start | bytes 196616 | tf_op jit(solution)/shard_map/ppermute | solution.py:361
  4.3 2.5 %collective-permute-start.1 = (bf16[4,2,2,16,128]{4,3,2,1,0:T(8,128)(2,1)S(1)}, bf16[4,2,2,16,128]{4,3,2,1,0:T(8,128)(2,1)S(1)}, u32[]{:S(2)}, u32[]{:S(2)}) collective-permute-start(bf16[4,2,2,16,128]{4,3,2,1,0:T(8,128)(2,1)S(1)} %bitcast.15), channel_id=1, source_target_pairs={{0,12},{4,8},{8,4},{12,0},{1,13},{5,9},{9,5},{13,1},{2,14},{6,10},... | collective-permute-start | bytes 196616 | tf_op jit(solution)/shard_map/ppermute | solution.py:361
  6.7 1.6 %collective-permute-start.2 = (bf16[4,2,2,16,128]{4,3,2,1,0:T(8,128)(2,1)S(1)}, bf16[4,2,2,16,128]{4,3,2,1,0:T(8,128)(2,1)S(1)}, u32[]{:S(2)}, u32[]{:S(2)}) collective-permute-start(bf16[4,2,2,16,128]{4,3,2,1,0:T(8,128)(2,1)S(1)} %bitcast.14), channel_id=1, source_target_pairs={{0,8},{4,0},{8,12},{12,4},{1,9},{5,1},{9,13},{13,5},{2,10},{6,2},{... | collective-permute-start | bytes 196616 | tf_op jit(solution)/shard_map/ppermute | solution.py:361
  8.3 2.2 %prepare.1 = (bf16[2,8,256,128]{3,2,1,0:T(8,128)(2,1)S(1)}, bf16[2,8,128,128]{3,2,1,0:T(8,128)(2,1)S(1)}, bf16[2,4,256,128]{3,2,1,0:T(8,128)(2,1)S(1)}, bf16[2,2...) custom-call(s32[1,2]{1,0:T(1,128)} %bitcast.19, ...), custom_call_target="tpu_custom_call" | custom-call | flops 1000000000 | bytes 4000000 | tf_op jit(solution)/shard_map/prepare/pallas_call | solution.py:312
  10.5 0.7 %collective-permute-done.1.refs_0_.refs_2_ = bf16[4,2,2,16,128]{4,3,2,1,0:T(8,128)(2,1)S(1)} collective-permute-done((bf16[4,2,2,16,128]{4,3,2,1,0:T(8,128)(2,1)S(1)}, bf16[4,2,2,16,128]{4,3,2,1,0:T(8,128)(2,1)S(1)}, u32[]{:S(2)}, u32[]{:S(2)}) %collective-permute-start.1) | collective-permute-done | bytes 65568 | tf_op jit(solution)/shard_map/ppermute | solution.py:361
  11.2 0.2 %collective-permute-done.2.refs_1_.refs_3_ = bf16[4,2,2,16,128]{4,3,2,1,0:T(8,128)(2,1)S(1)} collective-permute-done((bf16[4,2,2,16,128]{4,3,2,1,0:T(8,128)(2,1)S(1)}, bf16[4,2,2,16,128]{4,3,2,1,0:T(8,128)(2,1)S(1)}, u32[]{:S(2)}, u32[]{:S(2)}) %collective-permute-start.2) | collective-permute-done | bytes 65568 | tf_op jit(solution)/shard_map/ppermute | solution.py:361
  11.4 0.0 collective-permute-start.4
  11.5 0.0 collective-permute-done.refs_1_
  11.5 0.6 %collective-permute-start.3 = (bf16[4,2,2,16,128]{4,3,2,1,0:T(8,128)(2,1)S(1)}, bf16[4,2,2,16,128]{4,3,2,1,0:T(8,128)(2,1)S(1)}, u32[]{:S(2)}, u32[]{:S(2)}) collective-permute-start(bf16[4,2,2,16,128]{4,3,2,1,0:T(8,128)(2,1)S(1)} %join.2), channel_id=1, source_target_pairs={{0,1},{1,0},{2,3},{3,2},{4,5},{5,4},{6,7},{7,6},{8,9},{9,8},{10,11... | collective-permute-start | bytes 196616 | tf_op jit(solution)/shard_map/ppermute | solution.py:377
  12.0 0.7 %collective-permute-done.4 = bf16[4,2,2,16,128]{4,3,2,1,0:T(8,128)(2,1)S(1)} collective-permute-done((bf16[4,2,2,16,128]{4,3,2,1,0:T(8,128)(2,1)S(1)}, bf16[4,2,2,16,128]{4,3,2,1,0:T(8,128)(2,1)S(1)}, u32[]{:S(2)}, u32[]{:S(2)}) %collective-permute-start.4) | collective-permute-done | bytes 65568 | tf_op jit(solution)/shard_map/ppermute | solution.py:377
  12.7 0.2 %collective-permute-done.3 = bf16[4,2,2,16,128]{4,3,2,1,0:T(8,128)(2,1)S(1)} collective-permute-done((bf16[4,2,2,16,128]{4,3,2,1,0:T(8,128)(2,1)S(1)}, bf16[4,2,2,16,128]{4,3,2,1,0:T(8,128)(2,1)S(1)}, u32[]{:S(2)}, u32[]{:S(2)}) %collective-permute-start.3) | collective-permute-done | bytes 65568 | tf_op jit(solution)/shard_map/ppermute | solution.py:377
  12.9 4.2 %profiles.1 = bf16[2,2,512,256]{3,2,1,0:T(8,128)(2,1)} custom-call(bf16[2,2,2,16,128]{4,3,2,1,0:T(8,128)(2,1)S(1)} %bitcast.17, bf16[4,2,2,16,128]{4,3,2,1,0:T(8,128)(2,1)S(1)} %collective-permute-done.refs_1_, bf16[4,2,2,16,128]{4,3,2,1,0:T(8,128)(2,1)S(1)} %collective-permute-done.1.refs_0_.refs_2_, ...), custom_call_target="tpu_custom_call" | custom-call | flops 2000000000 | bytes 4000000 | tf_op jit(solution)/shard_map/profiles/pallas_call | solution.py:399
  (2 shorter events, 0.0 us)
Async XLA Ops:
  1.2 10.3 %collective-permute-start = (bf16[4,2,2,16,128]{4,3,2,1,0:T(8,128)(2,1)S(1)}, bf16[4,2,2,16,128]{4,3,2,1,0:T(8,128)(2,1)S(1)}, u32[]{:S(2)}, u32[]{:S(2)}) collective-permute-start(bf16[4,2,2,16,128]{4,3,2,1,0:T(8,128)(2,1)S(1)} %bitcast.12), channel_id=1, source_target_pairs={{0,4},{4,12},{8,0},{12,8},{1,5},{5,13},{9,1},{13,9},{2,6},{6,14},{... | collective-permute-start | bytes 196616 | tf_op jit(solution)/shard_map/ppermute | solution.py:361
  4.3 7.0 %collective-permute-start.1 = (bf16[4,2,2,16,128]{4,3,2,1,0:T(8,128)(2,1)S(1)}, bf16[4,2,2,16,128]{4,3,2,1,0:T(8,128)(2,1)S(1)}, u32[]{:S(2)}, u32[]{:S(2)}) collective-permute-start(bf16[4,2,2,16,128]{4,3,2,1,0:T(8,128)(2,1)S(1)} %bitcast.15), channel_id=1, source_target_pairs={{0,12},{4,8},{8,4},{12,0},{1,13},{5,9},{9,5},{13,1},{2,14},{6,10},... | collective-permute-start | bytes 196616 | tf_op jit(solution)/shard_map/ppermute | solution.py:361
  6.7 4.7 %collective-permute-start.2 = (bf16[4,2,2,16,128]{4,3,2,1,0:T(8,128)(2,1)S(1)}, bf16[4,2,2,16,128]{4,3,2,1,0:T(8,128)(2,1)S(1)}, u32[]{:S(2)}, u32[]{:S(2)}) collective-permute-start(bf16[4,2,2,16,128]{4,3,2,1,0:T(8,128)(2,1)S(1)} %bitcast.14), channel_id=1, source_target_pairs={{0,8},{4,0},{8,12},{12,4},{1,9},{5,1},{9,13},{13,5},{2,10},{6,2},{... | collective-permute-start | bytes 196616 | tf_op jit(solution)/shard_map/ppermute | solution.py:361
  11.4 1.3 %collective-permute-start.4 = (bf16[4,2,2,16,128]{4,3,2,1,0:T(8,128)(2,1)S(1)}, bf16[4,2,2,16,128]{4,3,2,1,0:T(8,128)(2,1)S(1)}, u32[]{:S(2)}, u32[]{:S(2)}) collective-permute-start(bf16[4,2,2,16,128]{4,3,2,1,0:T(8,128)(2,1)S(1)} %join.3), channel_id=1, source_target_pairs={{0,1},{1,0},{2,3},{3,2},{4,5},{5,4},{6,7},{7,6},{8,9},{9,8},{10,11... | collective-permute-start | bytes 196616 | tf_op jit(solution)/shard_map/ppermute | solution.py:377
  11.5 1.5 %collective-permute-start.3 = (bf16[4,2,2,16,128]{4,3,2,1,0:T(8,128)(2,1)S(1)}, bf16[4,2,2,16,128]{4,3,2,1,0:T(8,128)(2,1)S(1)}, u32[]{:S(2)}, u32[]{:S(2)}) collective-permute-start(bf16[4,2,2,16,128]{4,3,2,1,0:T(8,128)(2,1)S(1)} %join.2), channel_id=1, source_target_pairs={{0,1},{1,0},{2,3},{3,2},{4,5},{5,4},{6,7},{7,6},{8,9},{9,8},{10,11... | collective-permute-start | bytes 196616 | tf_op jit(solution)/shard_map/ppermute | solution.py:377

commit v6 on v5

--- a/solution.py
+++ b/solution.py
@@ -36,11 +36,17 @@
 
 def relay_kernel(places, x_ref, *refs):
     chunks, stack_ref, sem = refs[:-2], refs[-2], refs[-1]
-    whole = pltpu.make_async_copy(x_ref, stack_ref, sem)
-    whole.start()
+    parts = [
+        pltpu.make_async_copy(x_ref.at[half, at], stack_ref.at[half, at], sem)
+        for half in range(x_ref.shape[0])
+        for at in range(x_ref.shape[1])
+    ]
+    for part in parts:
+        part.start()
     chip, core = lax.axis_index("az"), lax.axis_index("acq")
     cores = lax.axis_size("acq")
-    whole.wait()
+    for part in parts:
+        part.wait()
     cut(places, chip, core, cores, stack_ref, chunks)
 
 
@@ -242,9 +248,9 @@
         ]
 
     for r in range(columns):
-        for a in range(blocks):
-            rows = slice(a * per_block, (a + 1) * per_block)
-            for slab in range(slabs):
+        for slab in range(slabs):
+            for a in range(blocks):
+                rows = slice(a * per_block, (a + 1) * per_block)
                 xr, xi = real_ref[r, slab, rows], imag_ref[r, slab, rows]
                 strength = (xr * xr + xi * xi).astype(BF16)
                 placed = dot(

time: 17.3 us -> 17.3 us (level)
  no operation moved by 1% of the time
where the time goes in v6:
time: 17.3 us; the launch traced here: 17.1 us
  starting transfers between devices  7.71 us (45%)
  Pallas kernels  7.5 us (43%)
  waiting for transfers between devices  1.83 us (11%)
    ppermute x3, starting transfers between devices, shards(): arrived = lax.ppermute(chunk, 'az', list(enumerate(targets)))  7.16 us
    pallas_call x1, Pallas kernels, shards(): pl.pallas_call(body, out_shape=jax.ShapeDtypeStruct((blocks, columns, ele...  4.21 us
    pallas_call x1, Pallas kernels, prepare(): pl.pallas_call(lambda *refs: prepare_kernel(acq_share, pairwise, *refs),...  2.2 us
    pallas_call x1, Pallas kernels, shards(): pl.pallas_call(lambda *refs: relay_kernel(places, *refs), out_shape=outpu...  1.08 us
    ppermute x3, waiting for transfers between devices, shards(): arrived = lax.ppermute(chunk, 'az', list(enumerate(targets)))  0.93 us
    ppermute x2, waiting for transfers between devices, shards(): array = lax.ppermute(passing, 'acq', [(0, 1), (1, 0)])  0.9 us
    ppermute x2, starting transfers between devices, shards(): array = lax.ppermute(passing, 'acq', [(0, 1), (1, 0)])  0.56 us
  transfers between devices with their start and end apart: 5, of which 4 were waited for; matrix products, arithmetic and copies ran while one was open for 0% of the time, Pallas kernels for 13%

profile of v6, /device:TPU:0, one launch (start us, length us, event | category | flops | bytes accessed | tf_op | source)
XLA Modules:
  0.0 17.1 jit_solution(4058797894699902236)
XLA Ops:
  0.0 1.1 %relay.1 = (bf16[2,2,2,8,2,128]{5,4,3,2,1,0:T(2,128)(2,1)S(1)}, bf16[2,2,2,8,2,128]{5,4,3,2,1,0:T(2,128)(2,1)S(1)}, bf16[4,2,2,8,2,128]{5,4,3,2,1,0:T(2,128)(2,1...) custom-call(bf16[2,8,16,2,2,128]{5,4,3,2,1,0:T(2,128)(2,1)} %bitcast.18), custom_call_target="tpu_custom_call" | custom-call | tf_op jit(solution)/shard_map/relay/pallas_call | solution.py:353
  1.1 3.1 %collective-permute-start = (bf16[4,2,2,16,128]{4,3,2,1,0:T(8,128)(2,1)S(1)}, bf16[4,2,2,16,128]{4,3,2,1,0:T(8,128)(2,1)S(1)}, u32[]{:S(2)}, u32[]{:S(2)}) collective-permute-start(bf16[4,2,2,16,128]{4,3,2,1,0:T(8,128)(2,1)S(1)} %bitcast.12), channel_id=1, source_target_pairs={{0,4},{4,12},{8,0},{12,8},{1,5},{5,13},{9,1},{13,9},{2,6},{6,14},{... | collective-permute-start | bytes 196616 | tf_op jit(solution)/shard_map/ppermute | solution.py:367
  4.2 2.5 %collective-permute-start.1 = (bf16[4,2,2,16,128]{4,3,2,1,0:T(8,128)(2,1)S(1)}, bf16[4,2,2,16,128]{4,3,2,1,0:T(8,128)(2,1)S(1)}, u32[]{:S(2)}, u32[]{:S(2)}) collective-permute-start(bf16[4,2,2,16,128]{4,3,2,1,0:T(8,128)(2,1)S(1)} %bitcast.15), channel_id=1, source_target_pairs={{0,12},{4,8},{8,4},{12,0},{1,13},{5,9},{9,5},{13,1},{2,14},{6,10},... | collective-permute-start | bytes 196616 | tf_op jit(solution)/shard_map/ppermute | solution.py:367
  6.7 1.6 %collective-permute-start.2 = (bf16[4,2,2,16,128]{4,3,2,1,0:T(8,128)(2,1)S(1)}, bf16[4,2,2,16,128]{4,3,2,1,0:T(8,128)(2,1)S(1)}, u32[]{:S(2)}, u32[]{:S(2)}) collective-permute-start(bf16[4,2,2,16,128]{4,3,2,1,0:T(8,128)(2,1)S(1)} %bitcast.14), channel_id=1, source_target_pairs={{0,8},{4,0},{8,12},{12,4},{1,9},{5,1},{9,13},{13,5},{2,10},{6,2},{... | collective-permute-start | bytes 196616 | tf_op jit(solution)/shard_map/ppermute | solution.py:367
  8.3 2.2 %prepare.1 = (bf16[2,8,256,128]{3,2,1,0:T(8,128)(2,1)S(1)}, bf16[2,8,128,128]{3,2,1,0:T(8,128)(2,1)S(1)}, bf16[2,4,256,128]{3,2,1,0:T(8,128)(2,1)S(1)}, bf16[2,2...) custom-call(s32[1,2]{1,0:T(1,128)} %bitcast.19, ...), custom_call_target="tpu_custom_call" | custom-call | flops 1000000000 | bytes 4000000 | tf_op jit(solution)/shard_map/prepare/pallas_call | solution.py:318
  10.5 0.7 %collective-permute-done.1.refs_0_.refs_2_ = bf16[4,2,2,16,128]{4,3,2,1,0:T(8,128)(2,1)S(1)} collective-permute-done((bf16[4,2,2,16,128]{4,3,2,1,0:T(8,128)(2,1)S(1)}, bf16[4,2,2,16,128]{4,3,2,1,0:T(8,128)(2,1)S(1)}, u32[]{:S(2)}, u32[]{:S(2)}) %collective-permute-start.1) | collective-permute-done | bytes 65568 | tf_op jit(solution)/shard_map/ppermute | solution.py:367
  11.2 0.2 %collective-permute-done.2.refs_1_.refs_3_ = bf16[4,2,2,16,128]{4,3,2,1,0:T(8,128)(2,1)S(1)} collective-permute-done((bf16[4,2,2,16,128]{4,3,2,1,0:T(8,128)(2,1)S(1)}, bf16[4,2,2,16,128]{4,3,2,1,0:T(8,128)(2,1)S(1)}, u32[]{:S(2)}, u32[]{:S(2)}) %collective-permute-start.2) | collective-permute-done | bytes 65568 | tf_op jit(solution)/shard_map/ppermute | solution.py:367
  11.4 0.0 collective-permute-start.4
  11.4 0.0 collective-permute-done.refs_1_
  11.4 0.6 %collective-permute-start.3 = (bf16[4,2,2,16,128]{4,3,2,1,0:T(8,128)(2,1)S(1)}, bf16[4,2,2,16,128]{4,3,2,1,0:T(8,128)(2,1)S(1)}, u32[]{:S(2)}, u32[]{:S(2)}) collective-permute-start(bf16[4,2,2,16,128]{4,3,2,1,0:T(8,128)(2,1)S(1)} %join.2), channel_id=1, source_target_pairs={{0,1},{1,0},{2,3},{3,2},{4,5},{5,4},{6,7},{7,6},{8,9},{9,8},{10,11... | collective-permute-start | bytes 196616 | tf_op jit(solution)/shard_map/ppermute | solution.py:383
  12.0 0.7 %collective-permute-done.4 = bf16[4,2,2,16,128]{4,3,2,1,0:T(8,128)(2,1)S(1)} collective-permute-done((bf16[4,2,2,16,128]{4,3,2,1,0:T(8,128)(2,1)S(1)}, bf16[4,2,2,16,128]{4,3,2,1,0:T(8,128)(2,1)S(1)}, u32[]{:S(2)}, u32[]{:S(2)}) %collective-permute-start.4) | collective-permute-done | bytes 65568 | tf_op jit(solution)/shard_map/ppermute | solution.py:383
  12.6 0.2 %collective-permute-done.3 = bf16[4,2,2,16,128]{4,3,2,1,0:T(8,128)(2,1)S(1)} collective-permute-done((bf16[4,2,2,16,128]{4,3,2,1,0:T(8,128)(2,1)S(1)}, bf16[4,2,2,16,128]{4,3,2,1,0:T(8,128)(2,1)S(1)}, u32[]{:S(2)}, u32[]{:S(2)}) %collective-permute-start.3) | collective-permute-done | bytes 65568 | tf_op jit(solution)/shard_map/ppermute | solution.py:383
  12.9 4.2 %profiles.1 = bf16[2,2,512,256]{3,2,1,0:T(8,128)(2,1)} custom-call(bf16[2,2,2,16,128]{4,3,2,1,0:T(8,128)(2,1)S(1)} %bitcast.17, bf16[4,2,2,16,128]{4,3,2,1,0:T(8,128)(2,1)S(1)} %collective-permute-done.refs_1_, bf16[4,2,2,16,128]{4,3,2,1,0:T(8,128)(2,1)S(1)} %collective-permute-done.1.refs_0_.refs_2_, ...), custom_call_target="tpu_custom_call" | custom-call | flops 2000000000 | bytes 4000000 | tf_op jit(solution)/shard_map/profiles/pallas_call | solution.py:405
  (2 shorter events, 0.0 us)
Async XLA Ops:
  1.1 10.3 %collective-permute-start = (bf16[4,2,2,16,128]{4,3,2,1,0:T(8,128)(2,1)S(1)}, bf16[4,2,2,16,128]{4,3,2,1,0:T(8,128)(2,1)S(1)}, u32[]{:S(2)}, u32[]{:S(2)}) collective-permute-start(bf16[4,2,2,16,128]{4,3,2,1,0:T(8,128)(2,1)S(1)} %bitcast.12), channel_id=1, source_target_pairs={{0,4},{4,12},{8,0},{12,8},{1,5},{5,13},{9,1},{13,9},{2,6},{6,14},{... | collective-permute-start | bytes 196616 | tf_op jit(solution)/shard_map/ppermute | solution.py:367
  4.2 7.0 %collective-permute-start.1 = (bf16[4,2,2,16,128]{4,3,2,1,0:T(8,128)(2,1)S(1)}, bf16[4,2,2,16,128]{4,3,2,1,0:T(8,128)(2,1)S(1)}, u32[]{:S(2)}, u32[]{:S(2)}) collective-permute-start(bf16[4,2,2,16,128]{4,3,2,1,0:T(8,128)(2,1)S(1)} %bitcast.15), channel_id=1, source_target_pairs={{0,12},{4,8},{8,4},{12,0},{1,13},{5,9},{9,5},{13,1},{2,14},{6,10},... | collective-permute-start | bytes 196616 | tf_op jit(solution)/shard_map/ppermute | solution.py:367
  6.7 4.7 %collective-permute-start.2 = (bf16[4,2,2,16,128]{4,3,2,1,0:T(8,128)(2,1)S(1)}, bf16[4,2,2,16,128]{4,3,2,1,0:T(8,128)(2,1)S(1)}, u32[]{:S(2)}, u32[]{:S(2)}) collective-permute-start(bf16[4,2,2,16,128]{4,3,2,1,0:T(8,128)(2,1)S(1)} %bitcast.14), channel_id=1, source_target_pairs={{0,8},{4,0},{8,12},{12,4},{1,9},{5,1},{9,13},{13,5},{2,10},{6,2},{... | collective-permute-start | bytes 196616 | tf_op jit(solution)/shard_map/ppermute | solution.py:367
  11.4 1.3 %collective-permute-start.4 = (bf16[4,2,2,16,128]{4,3,2,1,0:T(8,128)(2,1)S(1)}, bf16[4,2,2,16,128]{4,3,2,1,0:T(8,128)(2,1)S(1)}, u32[]{:S(2)}, u32[]{:S(2)}) collective-permute-start(bf16[4,2,2,16,128]{4,3,2,1,0:T(8,128)(2,1)S(1)} %join.3), channel_id=1, source_target_pairs={{0,1},{1,0},{2,3},{3,2},{4,5},{5,4},{6,7},{7,6},{8,9},{9,8},{10,11... | collective-permute-start | bytes 196616 | tf_op jit(solution)/shard_map/ppermute | solution.py:383
  11.4 1.5 %collective-permute-start.3 = (bf16[4,2,2,16,128]{4,3,2,1,0:T(8,128)(2,1)S(1)}, bf16[4,2,2,16,128]{4,3,2,1,0:T(8,128)(2,1)S(1)}, u32[]{:S(2)}, u32[]{:S(2)}) collective-permute-start(bf16[4,2,2,16,128]{4,3,2,1,0:T(8,128)(2,1)S(1)} %join.2), channel_id=1, source_target_pairs={{0,1},{1,0},{2,3},{3,2},{4,5},{5,4},{6,7},{7,6},{8,9},{9,8},{10,11... | collective-permute-start | bytes 196616 | tf_op jit(solution)/shard_map/ppermute | solution.py:383
